TPU v7x, 256 devices: a whole 4x4x8 slice. The times are simulated.
256 devices in a mesh: gx: 8 (over z), gy: 8 (over y, core), gz: 4 (over x).
Axes of the slice: x: 4, y: 4, z: 8, core: 2. Of those that a mesh axis runs over, the one named last changes fastest.
Arguments:
- density: float32 [64, 64, 512], P('gx', 'gy', 'gz'), may hold values from 0.5 to 2
- base_velocity: float32 [3, 64, 64, 512], P(None, 'gx', 'gy', 'gz'), may hold values from -0.4 to 0.4
- cells: int32 [3, 65536], P(None, ('gx', 'gy', 'gz')), may hold values from 0 to 511, as said below
- offsets: float32 [3, 65536], P(None, ('gx', 'gy', 'gz')), may hold values from 0 to 1
- target: float32 [3, 65536], P(None, ('gx', 'gy', 'gz')), may hold values from -0.4 to 0.4
- stiffness: float32 [65536], P(('gx', 'gy', 'gz')), may hold values from 0.01 to 0.1
- counts: int32 [256], P(('gx', 'gy', 'gz')), may hold values from 1 to 256, as said below
Outputs:
- forces: float32 [3, 65536], P(None, ('gx', 'gy', 'gz'))
Inputs may be any that keep to these rules, and one draw needn't show every extreme that they name: `cells`: each marker's cell lies inside the lattice block of the device that holds its slot. `counts`: some device holds exactly 256 live markers in every draw.
All inputs are finite; a program needn't handle non-finite values.
Results may differ from a plain program's by a relative error of at most 0.0001.
Values sent between devices are 32-bit elements; how exact they have to be, the bound alone decides.
A program may use at most 64 MiB of HBM per device.

v0:
```python
import functools
import itertools

import jax
import jax.numpy as jnp
from jax import lax
from jax.experimental import pallas as pl
from jax.experimental.pallas import tpu as pltpu
from jax.sharding import PartitionSpec as P

ITERS = 3
MOST_DIRECT = 64
LOW, HIGH = 2, 3
MESH_ID = pl.DeviceIdType.MESH
AXES = ("gx", "gy", "gz")


def round_up(value, multiple):
    return -(-value // multiple) * multiple


def axis_groups(count):
    groups = {}
    for shift in (0, -1, 1):
        groups.setdefault(shift % count, []).append(shift)
    return list(groups.items())


def span(shifts, size):
    if shifts == [0]:
        return 1, size + 3
    if shifts == [-1]:
        return 0, 4
    if shifts == [1]:
        return size + 1, 4
    return 0, size + 5


def weights(fraction):
    root = jnp.sqrt(1.0 + 4.0 * fraction - 4.0 * fraction * fraction)
    near, far = 3.0 - 2.0 * fraction, 1.0 + 2.0 * fraction
    return ((near - root) / 8.0, (near + root) / 8.0, (far + root) / 8.0, (far - root) / 8.0)


def table(cell, four, shifts, size, first, rows):
    place = lax.broadcasted_iota(jnp.int32, (rows, cell.shape[1]), 0).astype(jnp.float32) + first
    total = None
    for shift in shifts:
        apart = place - (cell + (1.0 + shift * size))
        part = jnp.where(apart == 3.0, four[3], 0.0)
        for number in (2, 1, 0):
            part = jnp.where(apart == float(number), four[number], part)
        total = part if total is None else total + part
    return total


def split(value):
    high = value.astype(jnp.bfloat16)
    return high, (value - high.astype(jnp.float32)).astype(jnp.bfloat16)


def dot_nt(a, b):
    return lax.dot_general(a, b, (((1,), (1,)), ((), ())), preferred_element_type=jnp.float32)


def dot_nn(a, b):
    return lax.dot_general(a, b, (((1,), (0,)), ((), ())), preferred_element_type=jnp.float32)


def kernel(
    counts, sizes, block, marks, aux, out, fields, xbuf, ybuf, zpack, zbuf, nbuf, fbuf, rbuf, dbuf, txy, thi, tlo, whi, wlo, grid,
    nsend, nrecv, rsend, rrecv, dsend, drecv, hsend, hrecv,
):
    size_x, size_y, size_z = sizes
    cap = marks.shape[1]
    rows_y, lanes = fields.shape[2], fields.shape[3]
    assert 8 * (size_x + 5) <= size_z == lanes - size_z
    wide_x = size_x + 5
    groups = [axis_groups(count) for count in counts]
    slots = list(itertools.product(*[[offset for offset, _ in group] for group in groups]))
    me = [lax.axis_index(name) for name in AXES]
    sent = []

    def device(offset):
        return tuple(lax.rem(m + o, n) for m, o, n in zip(me, offset, counts))

    def negated(offset):
        return tuple((-o) % n for o, n in zip(offset, counts))

    peers = {slot for slot in slots if any(slot)}
    for axis, count in enumerate(counts):
        for step in range(1, count):
            peers.add(tuple(step if a == axis else 0 for a in range(3)))
    everyone = [o for o in itertools.product(*[range(n) for n in counts]) if any(o)]
    direct = len(everyone) < MOST_DIRECT
    peers = everyone if direct else sorted(peers)
    barrier = pltpu.get_barrier_semaphore()
    for peer in peers:
        pl.semaphore_signal(barrier, inc=1, device_id=device(peer), device_id_type=MESH_ID)
    pl.semaphore_wait(barrier, len(peers))

    def neighbour_copy(turn, number):
        return pltpu.make_async_remote_copy(
            src_ref=fbuf.at[turn - 1, 0] if turn else nbuf.at[0],
            dst_ref=fbuf.at[turn - 1, number] if turn else nbuf.at[number],
            send_sem=nsend.at[turn, number - 1],
            recv_sem=nrecv.at[turn, number - 1],
            device_id=device(negated(slots[number])),
            device_id_type=MESH_ID,
        )

    def send_round(turn):
        for number in sorted(range(1, len(slots)), key=lambda k: (slots[k][0] == 0, k)):
            copy = neighbour_copy(turn, number)
            copy.start()
            sent.append(copy)

    def wait_round(turn, off_x):
        for number in range(1, len(slots)):
            if slots[number][0] == off_x:
                neighbour_copy(turn, number).wait_recv()

    def sum_copy(turn, stage, step):
        axis = 2 - stage
        offset = tuple((-step) % counts[axis] if a == axis else 0 for a in range(3))
        return pltpu.make_async_remote_copy(
            src_ref=rbuf.at[turn, stage, 0],
            dst_ref=rbuf.at[turn, stage, step],
            send_sem=rsend.at[turn, stage, step - 1],
            recv_sem=rrecv.at[turn, stage, step - 1],
            device_id=device(offset),
            device_id_type=MESH_ID,
        )

    def send_sum(turn, stage, value):
        rbuf[turn, stage, 0] = value
        for step in range(1, counts[2 - stage]):
            copy = sum_copy(turn, stage, step)
            copy.start()
            sent.append(copy)

    def wait_sum(turn, stage):
        for step in range(1, counts[2 - stage]):
            sum_copy(turn, stage, step).wait_recv()
        total = rbuf[turn, stage, 0]
        for step in range(1, counts[2 - stage]):
            total = total + rbuf[turn, stage, step]
        return total

    def put(turn, vector):
        for c in range(3):
            for part in range(cap // 128):
                fbuf[turn - 1, 0, pl.ds(c * (cap // 128) + part, 1), :] = vector[
                    c : c + 1, part * 128 : part * 128 + 128
                ]

    def taken(turn, number, c):
        each = cap // 128
        return jnp.concatenate(
            [fbuf[turn - 1, number, pl.ds(c * each + part, 1), :] for part in range(each)], axis=1
        )

    def direct_copy(number):
        return pltpu.make_async_remote_copy(
            src_ref=dbuf.at[0],
            dst_ref=dbuf.at[number + 1],
            send_sem=dsend.at[number],
            recv_sem=drecv.at[number],
            device_id=device(negated(everyone[number])),
            device_id_type=MESH_ID,
        )

    def sum_directly(value):
        dbuf[0] = value
        for number in range(len(everyone)):
            copy = direct_copy(number)
            copy.start()
            sent.append(copy)
        for number in range(len(everyone)):
            direct_copy(number).wait_recv()
        return jnp.sum(dbuf[...], axis=0)

    offs_y = sorted({1 % counts[1], (-1) % counts[1]})
    offs_z = sorted({1 % counts[2], (-1) % counts[2]})

    def halo_copy(number, source, target, offset):
        return pltpu.make_async_remote_copy(
            src_ref=source,
            dst_ref=target,
            send_sem=hsend.at[number],
            recv_sem=hrecv.at[number],
            device_id=device(negated(offset)),
            device_id_type=MESH_ID,
        )

    def go(copies):
        for copy in copies:
            copy.start()
            sent.append(copy)

    low, high = pl.ds(0, LOW), pl.ds(LOW, HIGH)
    along_x = [
        halo_copy(0, block.at[:, pl.ds(size_x - LOW, LOW)], xbuf.at[:, low], (counts[0] - 1, 0, 0)),
        halo_copy(1, block.at[:, pl.ds(0, HIGH)], xbuf.at[:, high], (1, 0, 0)),
    ]
    along_y, relayed_y = [], []
    for k, off in enumerate(offs_y):
        here = (0, off, 0)
        along_y.append(halo_copy(2 + k, block, ybuf.at[k, :, pl.ds(LOW, size_x)], here))
        relayed_y.append(halo_copy(4 + k, xbuf.at[:, low], ybuf.at[k, :, low], here))
        relayed_y.append(
            halo_copy(6 + k, xbuf.at[:, high], ybuf.at[k, :, pl.ds(LOW + size_x, HIGH)], here)
        )
    along_z = [halo_copy(8 + k, zpack, zbuf.at[k], (0, 0, off)) for k, off in enumerate(offs_z)]

    def widen():
        for copy in along_y + relayed_y:
            copy.wait_recv()
        below = ybuf.at[offs_y.index((-1) % counts[1])]
        above = ybuf.at[offs_y.index(1 % counts[1])]
        lane = lax.broadcasted_iota(jnp.int32, (4, rows_y, size_z), 2)
        zero = jnp.zeros((4, rows_y - size_y - LOW - HIGH, size_z), jnp.float32)
        packed = jnp.zeros((4, rows_y, size_z), jnp.float32)
        for plane in range(wide_x):
            if plane < LOW:
                own = xbuf[:, plane]
            elif plane < LOW + size_x:
                own = block[:, plane - LOW]
            else:
                own = xbuf[:, plane - size_x]
            tall = jnp.concatenate(
                [below[:, plane][:, size_y - LOW :], own, above[:, plane][:, :HIGH], zero], axis=1
            )
            fields[:, plane, :, pl.ds(0, size_z)] = tall
            ends = jnp.where(lane < HIGH, tall, pltpu.roll(tall, LOW + HIGH, 2))
            at = 8 * plane
            inside = (lane >= at) & (lane < at + LOW + HIGH)
            packed = jnp.where(inside, pltpu.roll(ends, at, 2) if at else ends, packed)
        zpack[...] = packed
        go(along_z)
        for copy in along_z:
            copy.wait_recv()
        before = zbuf[offs_z.index((-1) % counts[2])]
        after = zbuf[offs_z.index(1 % counts[2])]
        for plane in range(wide_x):
            at = 8 * plane
            tall = pltpu.roll(fields[:, plane, :, pl.ds(0, size_z)], LOW, 2)
            first = pltpu.roll(before, (-(at + HIGH)) % size_z, 2)
            last = pltpu.roll(after, (LOW - at) % size_z, 2)
            fields[:, plane, :, pl.ds(0, size_z)] = jnp.where(lane < LOW, first, tall)
            tail = jnp.where(lane < LOW, tall, jnp.where(lane < LOW + HIGH, last, 0.0))
            fields[:, plane, :, pl.ds(size_z, lanes - size_z)] = tail

    go(along_x + along_y)
    nbuf[0] = marks[...]
    send_round(0)

    def build(xi, yi, zi):
        number = slots.index((groups[0][xi][0], groups[1][yi][0], groups[2][zi][0]))
        info = nbuf[number]
        cells = [info[k : k + 1] for k in range(3)]
        fours = [weights(info[k + 3 : k + 4]) for k in range(3)]
        block = (yi * len(groups[2]) + zi) * cap
        start, planes = span(groups[0][xi][1], size_x)
        first = start // 8 * 8
        tall = round_up(start + planes - first, 8)
        tab_x = table(cells[0], fours[0], groups[0][xi][1], size_x, float(first), tall)
        tab_y = table(cells[1], fours[1], groups[1][yi][1], size_y, 0.0, rows_y)
        for plane in range(planes):
            at = start - first + plane
            txy[xi, pl.ds(plane * rows_y, rows_y), pl.ds(block, cap)] = tab_x[at : at + 1] * tab_y
        shifts = groups[2][zi][1]
        start, planes = span(shifts, size_z)
        first = start // 16 * 16
        tall = round_up(start + planes - first, 16)
        tab_z = table(cells[2], fours[2], shifts, size_z, float(first), tall)
        high, low = split(tab_z)
        for ref, part in ((thi, high), (tlo, low)):
            if first:
                ref[xi, pl.ds(0, first), pl.ds(block, cap)] = jnp.zeros((first, cap), jnp.bfloat16)
            ref[xi, pl.ds(first, tall), pl.ds(block, cap)] = part
            rest = lanes - first - tall
            if rest:
                ref[xi, pl.ds(first + tall, rest), pl.ds(block, cap)] = jnp.zeros(
                    (rest, cap), jnp.bfloat16
                )

    start_own, planes_own = span(groups[0][0][1], size_x)

    def interpolate(field):
        rows = planes_own * rows_y
        high, low = split(field.reshape(3 * rows, lanes))
        z_high, z_low = thi[0, :, pl.ds(0, cap)], tlo[0, :, pl.ds(0, cap)]
        part = dot_nn(high, z_high) + dot_nn(low, z_high) + dot_nn(high, z_low)
        plane = txy[0, pl.ds(0, rows), pl.ds(0, cap)]
        return jnp.concatenate(
            [
                jnp.sum(part[c * rows : (c + 1) * rows] * plane, axis=0, keepdims=True)
                for c in range(3)
            ],
            axis=0,
        )

    def spread(turn):
        for xi, (off_x, shifts) in enumerate(groups[0]):
            start, planes = span(shifts, size_x)
            rows = planes * rows_y
            wait_round(turn, off_x)
            for yi, (off_y, _) in enumerate(groups[1]):
                for zi, (off_z, _) in enumerate(groups[2]):
                    number = slots.index((off_x, off_y, off_z))
                    block = (yi * len(groups[2]) + zi) * cap
                    plane = txy[xi, pl.ds(0, rows), pl.ds(block, cap)]
                    for c in range(3):
                        high, low = split(plane * taken(turn, number, c))
                        whi[pl.ds(c * rows, rows), pl.ds(block, cap)] = high
                        wlo[pl.ds(c * rows, rows), pl.ds(block, cap)] = low
            high, low = whi[pl.ds(0, 3 * rows), :], wlo[pl.ds(0, 3 * rows), :]
            part = dot_nt(high, thi[xi]) + dot_nt(low, thi[xi]) + dot_nt(high, tlo[xi])
            part = part.reshape(3, planes, rows_y, lanes)
            if xi == 0:
                if start > 0:
                    grid[:, pl.ds(0, start)] = jnp.zeros((3, start, rows_y, lanes), jnp.float32)
                rest = wide_x - start - planes
                if rest > 0:
                    grid[:, pl.ds(start + planes, rest)] = jnp.zeros(
                        (3, rest, rows_y, lanes), jnp.float32
                    )
                grid[:, pl.ds(start, planes)] = part
            else:
                grid[:, pl.ds(start, planes)] += part

    def shifted(value, by, axis):
        return pltpu.roll(value, by % value.shape[axis], axis)

    def both(value, axis):
        return shifted(value, -1, axis), shifted(value, 1, axis)

    def add(value, axis):
        up, down = both(value, axis)
        return up + down

    def sub(value, axis):
        up, down = both(value, axis)
        return up - down

    def respond():
        scale = fields[3]
        mx, my, mz = (scale * grid[c] for c in range(3))
        slope_y, slope_z = sub(my, 1), sub(mz, 2)
        sum_x = 2.0 * mx + add(mx, 1) + add(mx, 2)
        slope = slope_y + slope_z
        px = sum_x[2:] + sum_x[:-2] + slope[2:] - slope[:-2]
        slope_x = mx[2:] - mx[:-2]
        sum_y = (2.0 * my + add(my, 2))[1:-1] + my[2:] + my[:-2]
        py = add(sum_y, 1) + sub(slope_x + slope_z[1:-1], 1)
        sum_z = (2.0 * mz + add(mz, 1))[1:-1] + mz[2:] + mz[:-2]
        pz = add(sum_z, 2) + sub(slope_x + slope_y[1:-1], 2)
        half = scale[1:-1] * 0.5
        return jnp.stack(
            [half * (m[1:-1] + p * (1.0 / 12.0)) for m, p in ((mx, px), (my, py), (mz, pz))]
        )

    target, stiffness, live = aux[pl.ds(0, 3), :], aux[pl.ds(3, 1), :], aux[pl.ds(4, 1), :]

    def apply(turn, vector, summing=None):
        spread(turn)
        if summing is not None:
            send_sum(summing, 1, wait_sum(summing, 0))
        field = respond()
        if summing is not None:
            send_sum(summing, 2, wait_sum(summing, 1))
        return live * (interpolate(field) + stiffness * vector)

    def partial_sums(residual, image):
        folded = []
        for other in (residual, image):
            row = jnp.sum(residual * other, axis=0, keepdims=True)
            total = row[:, :128]
            for at in range(128, cap, 128):
                total = total + row[:, at : at + 128]
            folded.append(total)
        return jnp.concatenate(folded, axis=0)

    def totals(tile):
        return (
            jnp.sum(tile[0:1], axis=1, keepdims=True),
            jnp.sum(tile[1:2], axis=1, keepdims=True),
        )

    build(0, 0, 0)
    for copy in along_x:
        copy.wait_recv()
    go(relayed_y)
    for off_x, _ in groups[0]:
        wait_round(0, off_x)
    for xi, yi, zi in itertools.product(*[range(len(group)) for group in groups]):
        if (xi, yi, zi) != (0, 0, 0):
            build(xi, yi, zi)
    widen()
    residual = live * (target - interpolate(fields[pl.ds(0, 3), pl.ds(1, size_x + 3)]))
    put(1, residual)
    send_round(1)

    image = apply(1, residual)
    direction, along, along_image = residual, image, None
    answer = None
    norm_before = alpha = None
    for step in range(ITERS):
        sums = partial_sums(residual, image)
        if step + 1 < ITERS or not direct:
            send_sum(step, 0, sums)
        if step + 1 < ITERS:
            put(step + 2, image)
            send_round(step + 2)
            ahead = apply(step + 2, image, step)
            norm, product = totals(wait_sum(step, 2))
        elif direct:
            norm, product = totals(sum_directly(sums))
        else:
            send_sum(step, 1, wait_sum(step, 0))
            send_sum(step, 2, wait_sum(step, 1))
            norm, product = totals(wait_sum(step, 2))
        if step == 0:
            alpha = norm / product
            along_image = ahead
        else:
            ratio = norm / norm_before
            alpha = norm / (product - ratio * norm / alpha)
            direction = residual + ratio * direction
            if step + 1 < ITERS:
                along = image + ratio * along
                along_image = ahead + ratio * along_image
        answer = alpha * direction if answer is None else answer + alpha * direction
        norm_before = norm
        if step + 1 < ITERS:
            residual = residual - alpha * along
            image = image - alpha * along_image
    out[...] = answer
    for copy in sent:
        copy.wait_send()


def body(mesh_counts, density, base_velocity, cells, offsets, target, stiffness, counts):
    sizes = density.shape
    size_x, size_y, size_z = sizes
    cap = cells.shape[1]
    rows_y, lanes = round_up(size_y + 5, 16), round_up(size_z + 5, 128)
    anchor = jnp.stack([lax.axis_index(name) * size for name, size in zip(AXES, sizes)])
    local = (cells - anchor[:, None]).astype(jnp.float32)
    marks = jnp.concatenate([local, offsets, jnp.zeros((2, cap), jnp.float32)], axis=0)
    live = (jnp.arange(cap, dtype=jnp.int32) < counts[0]).astype(jnp.float32)
    aux = jnp.concatenate(
        [target, stiffness[None], live[None], jnp.zeros((3, cap), jnp.float32)], axis=0
    )
    stacked = jnp.concatenate([base_velocity, lax.rsqrt(density)[None]], axis=0)
    groups = [axis_groups(count) for count in mesh_counts]
    number = len(groups[0]) * len(groups[1]) * len(groups[2])
    width = len(groups[1]) * len(groups[2]) * cap
    tallest = max(span(shifts, size_x)[1] for _, shifts in groups[0])
    longest = max(mesh_counts)
    turns = ITERS + 1
    devices = mesh_counts[0] * mesh_counts[1] * mesh_counts[2]
    most = devices if devices <= MOST_DIRECT else 1
    return pl.pallas_call(
        functools.partial(kernel, mesh_counts, sizes),
        out_shape=jax.ShapeDtypeStruct((3, cap), jnp.float32),
        in_specs=[pl.BlockSpec(memory_space=pltpu.VMEM)] * 3,
        out_specs=pl.BlockSpec(memory_space=pltpu.VMEM),
        scratch_shapes=[
            pltpu.VMEM((4, size_x + 5, rows_y, lanes), jnp.float32),
            pltpu.VMEM((4, LOW + HIGH, size_y, size_z), jnp.float32),
            pltpu.VMEM((2, 4, size_x + 5, size_y, size_z), jnp.float32),
            pltpu.VMEM((4, rows_y, size_z), jnp.float32),
            pltpu.VMEM((2, 4, rows_y, size_z), jnp.float32),
            pltpu.VMEM((number, 8, cap), jnp.float32),
            pltpu.VMEM((ITERS, number, 3 * (cap // 128), 128), jnp.float32),
            pltpu.VMEM((ITERS, 3, longest, 2, 128), jnp.float32),
            pltpu.VMEM((most, 2, 128), jnp.float32),
            pltpu.VMEM((len(groups[0]), tallest * rows_y, width), jnp.float32),
            pltpu.VMEM((len(groups[0]), lanes, width), jnp.bfloat16),
            pltpu.VMEM((len(groups[0]), lanes, width), jnp.bfloat16),
            pltpu.VMEM((3 * tallest * rows_y, width), jnp.bfloat16),
            pltpu.VMEM((3 * tallest * rows_y, width), jnp.bfloat16),
            pltpu.VMEM((3, size_x + 5, rows_y, lanes), jnp.float32),
            pltpu.SemaphoreType.DMA((turns, number - 1)),
            pltpu.SemaphoreType.DMA((turns, number - 1)),
            pltpu.SemaphoreType.DMA((ITERS, 3, longest - 1)),
            pltpu.SemaphoreType.DMA((ITERS, 3, longest - 1)),
            pltpu.SemaphoreType.DMA((most,)),
            pltpu.SemaphoreType.DMA((most,)),
            pltpu.SemaphoreType.DMA((10,)),
            pltpu.SemaphoreType.DMA((10,)),
        ],
        compiler_params=pltpu.CompilerParams(
            collective_id=0, has_side_effects=True, vmem_limit_bytes=60 * 1024 * 1024
        ),
    )(stacked, marks, aux)


def solution(mesh):
    return jax.shard_map(
        functools.partial(body, tuple(mesh.shape[name] for name in AXES)),
        mesh=mesh,
        in_specs=(
            P("gx", "gy", "gz"),
            P(None, "gx", "gy", "gz"),
            P(None, ("gx", "gy", "gz")),
            P(None, ("gx", "gy", "gz")),
            P(None, ("gx", "gy", "gz")),
            P(("gx", "gy", "gz")),
            P(("gx", "gy", "gz")),
        ),
        out_specs=P(None, ("gx", "gy", "gz")),
        check_vma=False,
    )
```

profile of v0, /device:TPU:1, one launch (start us, length us, event | category | flops | bytes accessed | tf_op | source)
XLA Modules:
  0.0 98.1 jit_solution(6616981945246988918)
XLA Ops:
  0.0 0.8 rsqrt_bitcast_fusion
  0.8 1.6 %pad_maximum_fusion.block = f32[4,8,8,128]{3,2,1,0:T(8,128)} fusion(f32[1,8,8,128]{3,2,1,0:T(8,128)S(1)} %rsqrt_bitcast_fusion, f32[3,8,8,128]{3,2,1,0:T(8,128)} %param.8), kind=kLoop, calls=%fused_computation | loop fusion | flops 32768 | bytes 262144 | tf_op jit(solution)/shard_map/concatenate | solution.py:456
  2.3 0.0 copy-start
  2.3 0.1 pad_add_fusion
  2.4 0.6 copy-done
  3.0 0.1 subtract_convert_fusion
  3.1 0.1 pad.6.clone
  3.2 0.0 copy-start.2
  3.2 0.1 pad.3.clone
  3.2 0.0 copy-start.1
  3.9 0.0 copy-start.3
  3.9 0.0 copy-done.2
  3.9 0.0 copy-done.1
  4.0 0.7 copy-done.3
  4.6 0.7 maximum_maximum_fusion
  5.3 91.6 %shard_map.73 = f32[3,256]{1,0:T(4,128)} custom-call(f32[4,8,8,128]{3,2,1,0:T(8,128)} %pad_maximum_fusion.block, f32[8,256]{1,0:T(8,128)} %get-tuple-element.5.marks, f32[8,256]{1,0:T(8,128)} %get-tuple-element.6.aux), custom_call_target="tpu_custom_call" | custom-call | tf_op jit(solution)/shard_map/pallas_call | solution.py:465
  96.8 1.3 %copy.10 = f32[3,256]{1,0:T(4,128)} copy(f32[3,256]{1,0:T(4,128)} %shard_map.73) | data formatting | bytes 6144
  (3 shorter events, 0.0 us)
Async XLA Ops:
  2.3 0.7 copy-start
  3.2 0.8 copy-start.2
  3.2 0.7 copy-start.1
  3.9 0.7 copy-start.3
where the time goes:
time: 98.4 us; the launch traced here: 98.1 us
  Pallas kernels  91.6 us (93%)
  local copies, waits for them, and re-layouts  3.47 us (4%)
  other arithmetic  2.38 us (2%)
    pallas_call x1, Pallas kernels, body(): pl.pallas_call(functools.partial(kernel, mesh_counts, sizes), out_shape=j...  91.6 us
    unnamed x9, local copies, waits for them, and re-layouts  2.55 us

commit v1 on v0

--- a/solution.py
+++ b/solution.py
@@ -9,7 +9,6 @@
 from jax.sharding import PartitionSpec as P
 
 ITERS = 3
-MOST_DIRECT = 64
 LOW, HIGH = 2, 3
 MESH_ID = pl.DeviceIdType.MESH
 AXES = ("gx", "gy", "gz")
@@ -68,11 +67,13 @@
 
 
 def kernel(
-    counts, sizes, block, marks, aux, out, fields, xbuf, ybuf, zpack, zbuf, nbuf, fbuf, rbuf, dbuf, txy, thi, tlo, whi, wlo, grid,
-    nsend, nrecv, rsend, rrecv, dsend, drecv, hsend, hrecv,
+    counts, sizes, density, velocity, cells_in, offsets_in, target_in, stiffness_in, count_in, out,
+    block, cells_ref, offsets_ref, target_ref, stiffness_ref, count_ref,
+    fields, xbuf, ybuf, zpack, zbuf, nbuf, fbuf, rbuf, sbuf, txy, thi, tlo, whi, wlo, grid,
+    lsem, nsend, nrecv, rsend, rrecv, ssend, srecv, hsend, hrecv,
 ):
     size_x, size_y, size_z = sizes
-    cap = marks.shape[1]
+    cap = cells_ref.shape[1]
     rows_y, lanes = fields.shape[2], fields.shape[3]
     assert 8 * (size_x + 5) <= size_z == lanes - size_z
     wide_x = size_x + 5
@@ -87,17 +88,28 @@
     def negated(offset):
         return tuple((-o) % n for o, n in zip(offset, counts))
 
-    peers = {slot for slot in slots if any(slot)}
-    for axis, count in enumerate(counts):
-        for step in range(1, count):
-            peers.add(tuple(step if a == axis else 0 for a in range(3)))
-    everyone = [o for o in itertools.product(*[range(n) for n in counts]) if any(o)]
-    direct = len(everyone) < MOST_DIRECT
-    peers = everyone if direct else sorted(peers)
+    near = [o for o in itertools.product([0], range(counts[1]), range(counts[2])) if any(o)]
+    far = [(o, 0, 0) for o in range(1, counts[0])]
+    peers = sorted({slot for slot in slots if any(slot)} | set(near) | set(far))
+    loads = [
+        pltpu.make_async_copy(source, destination, lsem.at[k])
+        for k, (source, destination) in enumerate(
+            [
+                (cells_in, cells_ref),
+                (offsets_in, offsets_ref),
+                (density, block.at[3]),
+                (velocity, block.at[pl.ds(0, 3)]),
+                (target_in, target_ref),
+                (stiffness_in, stiffness_ref),
+                (count_in, count_ref),
+            ]
+        )
+    ]
+    for load in loads:
+        load.start()
     barrier = pltpu.get_barrier_semaphore()
     for peer in peers:
         pl.semaphore_signal(barrier, inc=1, device_id=device(peer), device_id_type=MESH_ID)
-    pl.semaphore_wait(barrier, len(peers))
 
     def neighbour_copy(turn, number):
         return pltpu.make_async_remote_copy(
@@ -120,32 +132,33 @@
             if slots[number][0] == off_x:
                 neighbour_copy(turn, number).wait_recv()
 
-    def sum_copy(turn, stage, step):
-        axis = 2 - stage
-        offset = tuple((-step) % counts[axis] if a == axis else 0 for a in range(3))
+    def sum_copy(turn, stage, number):
+        members, buffer, send, receive = ((near, rbuf, rsend, rrecv), (far, sbuf, ssend, srecv))[stage]
         return pltpu.make_async_remote_copy(
-            src_ref=rbuf.at[turn, stage, 0],
-            dst_ref=rbuf.at[turn, stage, step],
-            send_sem=rsend.at[turn, stage, step - 1],
-            recv_sem=rrecv.at[turn, stage, step - 1],
-            device_id=device(offset),
+            src_ref=buffer.at[turn, 0],
+            dst_ref=buffer.at[turn, number + 1],
+            send_sem=send.at[turn, number],
+            recv_sem=receive.at[turn, number],
+            device_id=device(negated(members[number])),
             device_id_type=MESH_ID,
         )
 
+    def away(offset):
+        return -sum(min(o, n - o) for o, n in zip(offset, counts))
+
     def send_sum(turn, stage, value):
-        rbuf[turn, stage, 0] = value
-        for step in range(1, counts[2 - stage]):
-            copy = sum_copy(turn, stage, step)
+        members, buffer = ((near, rbuf), (far, sbuf))[stage]
+        buffer[turn, 0] = value
+        for number in sorted(range(len(members)), key=lambda k: (away(members[k]), k)):
+            copy = sum_copy(turn, stage, number)
             copy.start()
             sent.append(copy)
 
     def wait_sum(turn, stage):
-        for step in range(1, counts[2 - stage]):
-            sum_copy(turn, stage, step).wait_recv()
-        total = rbuf[turn, stage, 0]
-        for step in range(1, counts[2 - stage]):
-            total = total + rbuf[turn, stage, step]
-        return total
+        members, buffer = ((near, rbuf), (far, sbuf))[stage]
+        for number in sorted(range(len(members)), key=lambda k: (-away(members[k]), k)):
+            sum_copy(turn, stage, number).wait_recv()
+        return jnp.sum(buffer[turn], axis=0)
 
     def put(turn, vector):
         for c in range(3):
@@ -159,26 +172,6 @@
         return jnp.concatenate(
             [fbuf[turn - 1, number, pl.ds(c * each + part, 1), :] for part in range(each)], axis=1
         )
-
-    def direct_copy(number):
-        return pltpu.make_async_remote_copy(
-            src_ref=dbuf.at[0],
-            dst_ref=dbuf.at[number + 1],
-            send_sem=dsend.at[number],
-            recv_sem=drecv.at[number],
-            device_id=device(negated(everyone[number])),
-            device_id_type=MESH_ID,
-        )
-
-    def sum_directly(value):
-        dbuf[0] = value
-        for number in range(len(everyone)):
-            copy = direct_copy(number)
-            copy.start()
-            sent.append(copy)
-        for number in range(len(everyone)):
-            direct_copy(number).wait_recv()
-        return jnp.sum(dbuf[...], axis=0)
 
     offs_y = sorted({1 % counts[1], (-1) % counts[1]})
     offs_z = sorted({1 % counts[2], (-1) % counts[2]})
@@ -251,10 +244,6 @@
             tail = jnp.where(lane < LOW, tall, jnp.where(lane < LOW + HIGH, last, 0.0))
             fields[:, plane, :, pl.ds(size_z, lanes - size_z)] = tail
 
-    go(along_x + along_y)
-    nbuf[0] = marks[...]
-    send_round(0)
-
     def build(xi, yi, zi):
         number = slots.index((groups[0][xi][0], groups[1][yi][0], groups[2][zi][0]))
         info = nbuf[number]
@@ -301,7 +290,7 @@
             axis=0,
         )
 
-    def spread(turn):
+    def spread(turn, polls):
         for xi, (off_x, shifts) in enumerate(groups[0]):
             start, planes = span(shifts, size_x)
             rows = planes * rows_y
@@ -329,6 +318,8 @@
                 grid[:, pl.ds(start, planes)] = part
             else:
                 grid[:, pl.ds(start, planes)] += part
+            if polls:
+                polls.pop(0)()
 
     def shifted(value, by, axis):
         return pltpu.roll(value, by % value.shape[axis], axis)
@@ -361,15 +352,12 @@
             [half * (m[1:-1] + p * (1.0 / 12.0)) for m, p in ((mx, px), (my, py), (mz, pz))]
         )
 
-    target, stiffness, live = aux[pl.ds(0, 3), :], aux[pl.ds(3, 1), :], aux[pl.ds(4, 1), :]
-
-    def apply(turn, vector, summing=None):
-        spread(turn)
-        if summing is not None:
-            send_sum(summing, 1, wait_sum(summing, 0))
+    def apply(turn, vector, polls=()):
+        polls = list(polls)
+        spread(turn, polls)
         field = respond()
-        if summing is not None:
-            send_sum(summing, 2, wait_sum(summing, 1))
+        for poll in polls:
+            poll()
         return live * (interpolate(field) + stiffness * vector)
 
     def partial_sums(residual, image):
@@ -388,7 +376,23 @@
             jnp.sum(tile[1:2], axis=1, keepdims=True),
         )
 
+    loads[0].wait()
+    loads[1].wait()
+    for k, size in enumerate(sizes):
+        nbuf[0, pl.ds(k, 1), :] = (cells_ref[pl.ds(k, 1), :] - me[k] * size).astype(jnp.float32)
+    nbuf[0, pl.ds(3, 3), :] = offsets_ref[...]
     build(0, 0, 0)
+    loads[2].wait()
+    loads[3].wait()
+    block[3] = lax.rsqrt(block[3])
+    pl.semaphore_wait(barrier, len(peers))
+    go(along_x + along_y)
+    send_round(0)
+    loads[4].wait()
+    loads[5].wait()
+    loads[6].wait()
+    target, stiffness = target_ref[...], stiffness_ref[...]
+    live = (lax.broadcasted_iota(jnp.int32, (1, cap), 1) < count_ref[0]).astype(jnp.float32)
     for copy in along_x:
         copy.wait_recv()
     go(relayed_y)
@@ -398,45 +402,37 @@
         if (xi, yi, zi) != (0, 0, 0):
             build(xi, yi, zi)
     widen()
-    residual = live * (target - interpolate(fields[pl.ds(0, 3), pl.ds(1, size_x + 3)]))
-    put(1, residual)
+    base = live * (target - interpolate(fields[pl.ds(0, 3), pl.ds(1, size_x + 3)]))
+    put(1, base)
     send_round(1)
-
-    image = apply(1, residual)
-    direction, along, along_image = residual, image, None
-    answer = None
-    norm_before = alpha = None
-    for step in range(ITERS):
-        sums = partial_sums(residual, image)
-        if step + 1 < ITERS or not direct:
-            send_sum(step, 0, sums)
-        if step + 1 < ITERS:
-            put(step + 2, image)
-            send_round(step + 2)
-            ahead = apply(step + 2, image, step)
-            norm, product = totals(wait_sum(step, 2))
-        elif direct:
-            norm, product = totals(sum_directly(sums))
-        else:
-            send_sum(step, 1, wait_sum(step, 0))
-            send_sum(step, 2, wait_sum(step, 1))
-            norm, product = totals(wait_sum(step, 2))
-        if step == 0:
-            alpha = norm / product
-            along_image = ahead
-        else:
-            ratio = norm / norm_before
-            alpha = norm / (product - ratio * norm / alpha)
-            direction = residual + ratio * direction
-            if step + 1 < ITERS:
-                along = image + ratio * along
-                along_image = ahead + ratio * along_image
-        answer = alpha * direction if answer is None else answer + alpha * direction
-        norm_before = norm
-        if step + 1 < ITERS:
-            residual = residual - alpha * along
-            image = image - alpha * along_image
-    out[...] = answer
+    first = apply(1, base)
+    put(2, first)
+    send_round(2)
+    send_sum(0, 0, partial_sums(base, first))
+    second = apply(2, first, [lambda: send_sum(0, 1, wait_sum(0, 0))])
+    put(3, second)
+    send_round(3)
+    norm, product = totals(wait_sum(0, 1))
+    alpha = norm / product
+    answer = alpha * base
+    residual, image = base - alpha * first, first - alpha * second
+    send_sum(1, 0, partial_sums(residual, image))
+    third = apply(3, second, [lambda: send_sum(1, 1, wait_sum(1, 0))])
+    again = second - alpha * third
+    norm_before, alpha_before = norm, alpha
+    norm, product = totals(wait_sum(1, 1))
+    ratio = norm / norm_before
+    alpha = norm / (product - ratio * norm / alpha_before)
+    direction = residual + ratio * base
+    answer = answer + alpha * direction
+    residual, image = residual - alpha * (image + ratio * first), image - alpha * (again + ratio * second)
+    send_sum(2, 0, partial_sums(residual, image))
+    send_sum(2, 1, wait_sum(2, 0))
+    norm_before, alpha_before = norm, alpha
+    norm, product = totals(wait_sum(2, 1))
+    ratio = norm / norm_before
+    alpha = norm / (product - ratio * norm / alpha_before)
+    out[...] = answer + alpha * (residual + ratio * direction)
     for copy in sent:
         copy.wait_send()
 
@@ -446,28 +442,24 @@
     size_x, size_y, size_z = sizes
     cap = cells.shape[1]
     rows_y, lanes = round_up(size_y + 5, 16), round_up(size_z + 5, 128)
-    anchor = jnp.stack([lax.axis_index(name) * size for name, size in zip(AXES, sizes)])
-    local = (cells - anchor[:, None]).astype(jnp.float32)
-    marks = jnp.concatenate([local, offsets, jnp.zeros((2, cap), jnp.float32)], axis=0)
-    live = (jnp.arange(cap, dtype=jnp.int32) < counts[0]).astype(jnp.float32)
-    aux = jnp.concatenate(
-        [target, stiffness[None], live[None], jnp.zeros((3, cap), jnp.float32)], axis=0
-    )
-    stacked = jnp.concatenate([base_velocity, lax.rsqrt(density)[None]], axis=0)
     groups = [axis_groups(count) for count in mesh_counts]
     number = len(groups[0]) * len(groups[1]) * len(groups[2])
     width = len(groups[1]) * len(groups[2]) * cap
     tallest = max(span(shifts, size_x)[1] for _, shifts in groups[0])
-    longest = max(mesh_counts)
     turns = ITERS + 1
-    devices = mesh_counts[0] * mesh_counts[1] * mesh_counts[2]
-    most = devices if devices <= MOST_DIRECT else 1
+    near, far = mesh_counts[1] * mesh_counts[2], mesh_counts[0]
     return pl.pallas_call(
         functools.partial(kernel, mesh_counts, sizes),
         out_shape=jax.ShapeDtypeStruct((3, cap), jnp.float32),
-        in_specs=[pl.BlockSpec(memory_space=pltpu.VMEM)] * 3,
+        in_specs=[pl.BlockSpec(memory_space=pltpu.HBM)] * 7,
         out_specs=pl.BlockSpec(memory_space=pltpu.VMEM),
         scratch_shapes=[
+            pltpu.VMEM((4, size_x, size_y, size_z), jnp.float32),
+            pltpu.VMEM((3, cap), jnp.int32),
+            pltpu.VMEM((3, cap), jnp.float32),
+            pltpu.VMEM((3, cap), jnp.float32),
+            pltpu.VMEM((1, cap), jnp.float32),
+            pltpu.SMEM((1,), jnp.int32),
             pltpu.VMEM((4, size_x + 5, rows_y, lanes), jnp.float32),
             pltpu.VMEM((4, LOW + HIGH, size_y, size_z), jnp.float32),
             pltpu.VMEM((2, 4, size_x + 5, size_y, size_z), jnp.float32),
@@ -475,27 +467,28 @@
             pltpu.VMEM((2, 4, rows_y, size_z), jnp.float32),
             pltpu.VMEM((number, 8, cap), jnp.float32),
             pltpu.VMEM((ITERS, number, 3 * (cap // 128), 128), jnp.float32),
-            pltpu.VMEM((ITERS, 3, longest, 2, 128), jnp.float32),
-            pltpu.VMEM((most, 2, 128), jnp.float32),
+            pltpu.VMEM((ITERS, near, 2, 128), jnp.float32),
+            pltpu.VMEM((ITERS, far, 2, 128), jnp.float32),
             pltpu.VMEM((len(groups[0]), tallest * rows_y, width), jnp.float32),
             pltpu.VMEM((len(groups[0]), lanes, width), jnp.bfloat16),
             pltpu.VMEM((len(groups[0]), lanes, width), jnp.bfloat16),
             pltpu.VMEM((3 * tallest * rows_y, width), jnp.bfloat16),
             pltpu.VMEM((3 * tallest * rows_y, width), jnp.bfloat16),
             pltpu.VMEM((3, size_x + 5, rows_y, lanes), jnp.float32),
+            pltpu.SemaphoreType.DMA((7,)),
             pltpu.SemaphoreType.DMA((turns, number - 1)),
             pltpu.SemaphoreType.DMA((turns, number - 1)),
-            pltpu.SemaphoreType.DMA((ITERS, 3, longest - 1)),
-            pltpu.SemaphoreType.DMA((ITERS, 3, longest - 1)),
-            pltpu.SemaphoreType.DMA((most,)),
-            pltpu.SemaphoreType.DMA((most,)),
+            pltpu.SemaphoreType.DMA((ITERS, near - 1)),
+            pltpu.SemaphoreType.DMA((ITERS, near - 1)),
+            pltpu.SemaphoreType.DMA((ITERS, far - 1)),
+            pltpu.SemaphoreType.DMA((ITERS, far - 1)),
             pltpu.SemaphoreType.DMA((10,)),
             pltpu.SemaphoreType.DMA((10,)),
         ],
         compiler_params=pltpu.CompilerParams(
             collective_id=0, has_side_effects=True, vmem_limit_bytes=60 * 1024 * 1024
         ),
-    )(stacked, marks, aux)
+    )(density, base_velocity, cells, offsets, target, stiffness[None], counts)
 
 
 def solution(mesh):

time: 98.4 us -> 76.4 us (0.78)
  Pallas kernels: 91.6 us -> 74.3 us
  other arithmetic: 2.38 us -> 0 us
  local copies, waits for them, and re-layouts: 3.47 us -> 1.28 us
    pallas_call x1, Pallas kernels: 91.6 us -> 74.3 us  [body(): pl.pallas_call(functools.partial(kernel, mesh_counts, sizes), out_shape=j...]
    concatenate x2 -> x0, other arithmetic: 2.23 us -> none  [the longest x1 1.56 us: body(): stacked = jnp.concatenate([base_velocity, lax.rsqrt(density)[None]], axis=0)]
    unnamed x9 -> x1, local copies, waits for them, and re-layouts: 2.55 us -> 1.28 us
where the time goes in v1:
time: 76.4 us; the launch traced here: 76.3 us
  Pallas kernels  74.3 us (97%)
  local copies, waits for them, and re-layouts  1.28 us (2%)
    pallas_call x1, Pallas kernels, body(): pl.pallas_call(functools.partial(kernel, mesh_counts, sizes), out_shape=j...  74.3 us

profile of v1, /device:TPU:1, one launch (start us, length us, event | category | flops | bytes accessed | tf_op | source)
XLA Modules:
  0.0 76.3 jit_solution(17246182786566955915)
XLA Ops:
  0.7 74.3 %shard_map.73 = f32[3,256]{1,0:T(4,128)} custom-call(f32[8,8,128]{2,1,0:T(8,128)} %density.1, f32[3,8,8,128]{3,2,1,0:T(8,128)} %velocity.1, s32[3,256]{1,0:T(4,128)} %cells_in.1, f32[3,256]{1,0:T(4,128)} %offsets_in.1, f32[3,256]{1,0:T(4,128)} %target_in.1, f32[1,256]{1,0:T(1,128)} %bitcast.1, s32[1]{0:T(128)S(6)} %copy.9.count_in), custom_call_target="tpu_custom_call" | custom-call | tf_op jit(solution)/shard_map/pallas_call | solution.py:451
  75.0 1.3 %copy.10 = f32[3,256]{1,0:T(4,128)} copy(f32[3,256]{1,0:T(4,128)} %shard_map.73) | data formatting | bytes 6144

commit v2 on v1

v2 whole, which is shorter than its diff:
```python
import functools
import itertools

import jax
import jax.numpy as jnp
from jax import lax
from jax.experimental import pallas as pl
from jax.experimental.pallas import tpu as pltpu
from jax.sharding import PartitionSpec as P

ITERS = 3
LOW, HIGH = 2, 3
WIDE, TALL, HALF = 13, 16, 8
STEPS = (0, -1, 1)
MESH_ID = pl.DeviceIdType.MESH
AXES = ("gx", "gy", "gz")


def round_up(value, multiple):
    return -(-value // multiple) * multiple


def span(shift, size):
    return {0: (1, size + 3), -1: (0, 4), 1: (size + 1, 4)}[shift]


def weights(fraction):
    root = jnp.sqrt(1.0 + 4.0 * fraction - 4.0 * fraction * fraction)
    near, far = 3.0 - 2.0 * fraction, 1.0 + 2.0 * fraction
    return ((near - root) / 8.0, (near + root) / 8.0, (far + root) / 8.0, (far - root) / 8.0)


def table(cell, four, shift, size, first, rows):
    place = lax.broadcasted_iota(jnp.int32, (rows, cell.shape[1]), 0).astype(jnp.float32) + first
    apart = place - (cell + (1.0 + shift * size))
    total = jnp.where(apart == 3.0, four[3], 0.0)
    for number in (2, 1, 0):
        total = jnp.where(apart == float(number), four[number], total)
    return total


def split(value):
    high = value.astype(jnp.bfloat16)
    return high, (value - high.astype(jnp.float32)).astype(jnp.bfloat16)


def dot_nt(a, b):
    return lax.dot_general(a, b, (((1,), (1,)), ((), ())), preferred_element_type=jnp.float32)


def dot_nn(a, b):
    return lax.dot_general(a, b, (((1,), (0,)), ((), ())), preferred_element_type=jnp.float32)


def patches():
    found, base = {}, 0
    for step_x, step_y in itertools.product(STEPS, STEPS):
        row, rows = {0: (0, TALL), -1: (0, HALF), 1: (HALF, HALF)}[step_y]
        start, planes = span(step_x, 8)
        if step_x == 0 and step_y:
            planes += 1
        found[step_x, step_y] = (start, planes, row, rows, base)
        base += planes * rows
    return found, base


PATCHES, PATCH_ROWS = patches()
FLAT = list(PATCHES)


def kernel(
    counts, sizes, density, velocity, cells_in, offsets_in, target_in, stiffness_in, count_in, out,
    block, cells_ref, offsets_ref, target_ref, stiffness_ref, count_ref,
    fields, xbuf, ylow, yhigh, below, above, zlow, zhigh, zbuf, nbuf, fbuf, rbuf, sbuf,
    txy, thi, tlo, azz, tzz, edge, grid,
    lsem, nsend, nrecv, rsend, rrecv, ssend, srecv, hsend, hrecv,
):
    size_x, size_y, size_z = sizes
    cap = cells_ref.shape[1]
    lanes = fields.shape[3]
    slots = list(itertools.product(STEPS, STEPS, STEPS))
    me = [lax.axis_index(name) for name in AXES]
    sent = []

    def device(offset):
        return tuple(lax.rem(m + (o % n), n) for m, o, n in zip(me, offset, counts))

    def negated(offset):
        return tuple(-o for o in offset)

    near = [o for o in itertools.product([0], range(counts[1]), range(counts[2])) if any(o)]
    far = [(o, 0, 0) for o in range(1, counts[0])]
    wrapped = {tuple(o % n for o, n in zip(slot, counts)) for slot in slots if any(slot)}
    peers = sorted(wrapped | set(near) | set(far))
    loads = [
        pltpu.make_async_copy(source, destination, lsem.at[k])
        for k, (source, destination) in enumerate(
            [
                (velocity, block.at[pl.ds(0, 3)]),
                (density, block.at[3]),
                (cells_in, cells_ref),
                (offsets_in, offsets_ref),
                (target_in, target_ref),
                (stiffness_in, stiffness_ref),
                (count_in, count_ref),
            ]
        )
    ]
    for load in loads:
        load.start()
    barrier = pltpu.get_barrier_semaphore()
    for peer in peers:
        pl.semaphore_signal(barrier, inc=1, device_id=device(peer), device_id_type=MESH_ID)

    def go(copies):
        for copy in copies:
            copy.start()
            sent.append(copy)

    def neighbour_copy(turn, number):
        return pltpu.make_async_remote_copy(
            src_ref=fbuf.at[turn - 1, 0] if turn else nbuf.at[0],
            dst_ref=fbuf.at[turn - 1, number] if turn else nbuf.at[number],
            send_sem=nsend.at[turn, number - 1],
            recv_sem=nrecv.at[turn, number - 1],
            device_id=device(negated(slots[number])),
            device_id_type=MESH_ID,
        )

    def send_round(turn):
        far_first = sorted(range(1, len(slots)), key=lambda k: (-sum(map(abs, slots[k])), k))
        go([neighbour_copy(turn, number) for number in far_first])

    def wait_round(turn):
        for number in range(1, len(slots)):
            neighbour_copy(turn, number).wait_recv()

    def sum_copy(turn, stage, number):
        members, buffer, send, receive = ((near, rbuf, rsend, rrecv), (far, sbuf, ssend, srecv))[stage]
        return pltpu.make_async_remote_copy(
            src_ref=buffer.at[turn, 0],
            dst_ref=buffer.at[turn, number + 1],
            send_sem=send.at[turn, number],
            recv_sem=receive.at[turn, number],
            device_id=device(negated(members[number])),
            device_id_type=MESH_ID,
        )

    def away(offset):
        return -sum(min(o, n - o) for o, n in zip(offset, counts))

    def send_sum(turn, stage, value):
        members, buffer = ((near, rbuf), (far, sbuf))[stage]
        buffer[turn, 0] = value
        ordered = sorted(range(len(members)), key=lambda k: (away(members[k]), k))
        go([sum_copy(turn, stage, number) for number in ordered])

    def wait_sum(turn, stage):
        members, buffer = ((near, rbuf), (far, sbuf))[stage]
        for number in sorted(range(len(members)), key=lambda k: (-away(members[k]), k)):
            sum_copy(turn, stage, number).wait_recv()
        return jnp.sum(buffer[turn], axis=0)

    def put(turn, vector):
        for c in range(3):
            for part in range(cap // 128):
                fbuf[turn - 1, 0, pl.ds(c * (cap // 128) + part, 1), :] = vector[
                    c : c + 1, part * 128 : part * 128 + 128
                ]

    def joined(ref, at, number, k):
        each = cap // 128
        return jnp.concatenate(
            [ref[at, number, pl.ds(k * each + part, 1), :] for part in range(each)], axis=1
        )

    def mark(number, k):
        each = cap // 128
        parts = [divmod(k * each + part, 4) for part in range(each)]
        return jnp.concatenate([nbuf[number, a, pl.ds(b, 1), :] for a, b in parts], axis=1)

    def halo_copy(number, source, target, step):
        return pltpu.make_async_remote_copy(
            src_ref=source,
            dst_ref=target,
            send_sem=hsend.at[number],
            recv_sem=hrecv.at[number],
            device_id=device(negated(step)),
            device_id_type=MESH_ID,
        )

    flows, scalars = [], []
    plane_of = {-1: (size_x - LOW, LOW, 0), 1: (0, HIGH, LOW)}
    low_of = {-1: (1, 1, 0), 0: (0, 2, 1), 1: (0, 1, 3)}
    high_of = {-1: (3, 1, 0), 0: (0, 4, 1), 1: (0, 2, 5)}
    for copies, part in ((flows, pl.ds(0, 3)), (scalars, pl.ds(3, 1))):
        for step_x, step_y in sorted(FLAT, key=lambda o: -abs(o[0]) - abs(o[1])):
            if step_y:
                source, target, where = (
                    (ylow, below, low_of) if step_y < 0 else (yhigh, above, high_of)
                )
            elif step_x:
                source, target, where = block, xbuf, plane_of
            else:
                continue
            first, many, at = where[step_x]
            copies.append(
                halo_copy(
                    len(flows) + len(scalars),
                    source.at[part, pl.ds(first, many)],
                    target.at[part, pl.ds(at, many)],
                    (step_x, step_y, 0),
                )
            )
    edges = []
    for k, (step_x, step_y) in sorted(enumerate(FLAT), key=lambda o: -abs(o[1][0]) - abs(o[1][1])):
        for side, step_z in enumerate((-1, 1)):
            edges.append(
                halo_copy(
                    len(flows) + len(scalars) + len(edges),
                    (zlow, zhigh)[side],
                    zbuf.at[side, k],
                    (step_x, step_y, step_z),
                )
            )

    lane = lax.broadcasted_iota(jnp.int32, (size_y, size_z), 1)
    row = lax.broadcasted_iota(jnp.int32, (size_y, size_z), 0)

    def turned(value, by, axis):
        by %= value.shape[axis]
        return pltpu.roll(value, by, axis) if by else value

    def pack():
        low = [jnp.zeros((size_y, size_z), jnp.float32)] * 2
        high = [jnp.zeros((size_y, size_z), jnp.float32)] * 2
        for c in range(4):
            tiles_low = [None] * 2
            tiles_high = [None] * 4
            for plane in range(size_x):
                own = block[c, plane]
                t, q = divmod(plane, 4)
                moved = turned(own, 2 * q - 6, 0)
                tiles_low[t] = moved if q == 0 else jnp.where(row // 2 == q, moved, tiles_low[t])
                t, q = divmod(plane, 2)
                moved = turned(own, 4 * q, 0)
                tiles_high[t] = moved if q == 0 else jnp.where(row // 4 == q, moved, tiles_high[t])
                at = c * size_x + plane
                chain = plane % 2
                low[chain] = jnp.where(
                    lane // 2 == at, turned(own, 2 * at - (size_z - LOW), 1), low[chain]
                )
                high[chain] = jnp.where(lane // 4 == at, turned(own, 4 * at, 1), high[chain])
            for t in range(2):
                ylow[c, t] = tiles_low[t]
            for t in range(4):
                yhigh[c, t] = tiles_high[t]
        zlow[...] = jnp.where(lane // 2 % 2 == 0, low[0], low[1])
        zhigh[...] = jnp.where(lane // 4 % 2 == 0, high[0], high[1])

    def tall_of(down, own, up):
        moved = turned(own, LOW, 0)
        return (
            jnp.where(row < LOW, down, moved),
            jnp.where(row < LOW, moved, up),
        )

    def widen(components, first):
        sides = {}
        for step_x in STEPS:
            for side in range(2):
                down, own, up = (zbuf[side, FLAT.index((step_x, step_y))] for step_y in (-1, 0, 1))
                sides[step_x, side] = tall_of(turned(down, LOW, 0), own, turned(up, LOW, 0))
        for plane in range(WIDE):
            if plane < LOW:
                step_x, x = -1, plane + size_x - LOW
            elif plane < LOW + size_x:
                step_x, x = 0, plane - LOW
            else:
                step_x, x = 1, plane - LOW - size_x
            for c in components:
                own = block[c, x] if step_x == 0 else xbuf[c, plane if step_x < 0 else plane - size_x]
                source, _, at = low_of[step_x]
                down = turned(below[c, at + x // 4 - source], -2 * (x % 4), 0)
                source, _, at = high_of[step_x]
                up = turned(above[c, at + x // 2 - source], LOW - 4 * (x % 2), 0)
                talls = tall_of(down, own, up)
                index = c * size_x + x
                for half in range(2):
                    moved = turned(talls[half], LOW, 1)
                    start = turned(sides[step_x, 0][half], -2 * index, 1)
                    end = turned(sides[step_x, 1][half], LOW - 4 * index, 1)
                    left = jnp.where(lane < LOW, start, moved)
                    right = jnp.where(lane < LOW, moved, jnp.where(lane < LOW + HIGH, end, first))
                    if half:
                        left = jnp.where(row < LOW + HIGH, left, first)
                        right = jnp.where(row < LOW + HIGH, right, first)
                    if c == 3:
                        left, right = lax.rsqrt(left), lax.rsqrt(right)
                    rows = pl.ds(half * size_y, size_y)
                    fields[c, plane, rows, pl.ds(0, size_z)] = left
                    fields[c, plane, rows, pl.ds(size_z, size_z)] = right

    def tables(step_x, step_y, step_z):
        number = slots.index((step_x, step_y, step_z))
        cells = [mark(number, k) for k in range(3)]
        fours = [weights(mark(number, k + 3)) for k in range(3)]
        start, planes, first_row, rows, base = PATCHES[step_x, step_y]
        first = start // 8 * 8
        tall = round_up(start + planes - first, 8)
        tab_x = table(cells[0], fours[0], step_x, size_x, float(first), tall)
        tab_y = table(cells[1], fours[1], step_y, size_y, float(first_row), rows)
        return cells[2], fours[2], [
            tab_x[start - first + plane : start - first + plane + 1] * tab_y for plane in range(planes)
        ]

    def build_main(step_x, step_y):
        cell, four, products = tables(step_x, step_y, 0)
        start, planes, first_row, rows, base = PATCHES[step_x, step_y]
        for plane, product in enumerate(products):
            txy[pl.ds(base + plane * rows, rows), :] = product
        k = FLAT.index((step_x, step_y))
        used = round_up(size_z + 5, 16)
        high, low = split(table(cell, four, 0, size_z, 0.0, used))
        for ref, part in ((thi, high), (tlo, low)):
            ref[k, pl.ds(0, used), :] = part
            ref[k, pl.ds(used, lanes - used), :] = jnp.zeros((lanes - used, cap), jnp.bfloat16)

    def build_side(step_x, step_y, side):
        cell, four, products = tables(step_x, step_y, (-1, 1)[side])
        start, planes, first_row, rows, base = PATCHES[step_x, step_y]
        many = planes * rows
        high, low = split(jnp.concatenate(products, axis=0))
        azz[side, pl.ds(2 * base, many), :] = high
        azz[side, pl.ds(2 * base + many, many), :] = low
        k = FLAT.index((step_x, step_y))
        tzz[side, k] = table(cell, four, (-1, 1)[side], size_z, float(side * size_z), 8)

    _, own_planes, _, _, _ = PATCHES[0, 0]
    own_rows = own_planes * TALL

    def interpolate(field):
        high, low = split(field.reshape(3 * own_rows, lanes))
        z_high, z_low = thi[0], tlo[0]
        part = dot_nn(high, z_high) + dot_nn(low, z_high) + dot_nn(high, z_low)
        plane = txy[pl.ds(0, own_rows), :]
        return jnp.concatenate(
            [
                jnp.sum(part[c * own_rows : (c + 1) * own_rows] * plane, axis=0, keepdims=True)
                for c in range(3)
            ],
            axis=0,
        )

    def spread_main(turn, step_x, step_y):
        start, planes, first_row, rows, base = PATCHES[step_x, step_y]
        number = slots.index((step_x, step_y, 0))
        k = FLAT.index((step_x, step_y))
        plane = txy[pl.ds(base, planes * rows), :]
        high, low = split(
            jnp.concatenate([plane * joined(fbuf, turn - 1, number, c) for c in range(3)], axis=0)
        )
        part = dot_nt(high, thi[k]) + dot_nt(low, thi[k]) + dot_nt(high, tlo[k])
        part = part.reshape(3, planes, rows, lanes)
        if number == 0:
            for edge_plane in (0, WIDE - 1):
                grid[:, edge_plane] = jnp.zeros((3, TALL, lanes), jnp.float32)
            grid[:, pl.ds(start, planes)] = part
        else:
            grid[:, pl.ds(start, planes), pl.ds(first_row, rows)] += part

    def spread_side(turn, step_x, step_y, side):
        start, planes, first_row, rows, base = PATCHES[step_x, step_y]
        number = slots.index((step_x, step_y, (-1, 1)[side]))
        k = FLAT.index((step_x, step_y))
        many = planes * rows
        tab = tzz[side, k]
        pieces = [tab * joined(fbuf, turn - 1, number, c) for c in range(3)]
        high, low = split(jnp.concatenate(pieces + [jnp.zeros_like(tab)], axis=0))
        part = dot_nt(
            azz[side, pl.ds(2 * base, 2 * many), :], jnp.concatenate([high, low], axis=0)
        )
        part = (part[:many] + part[many:]).reshape(planes, rows, 64)
        where = (side, pl.ds(start, planes), pl.ds(first_row, rows), pl.ds(0, 64))
        if (step_x, step_y) == (0, 0):
            edge[where] = part
        else:
            edge[where] += part

    def finish_sides():
        inside = lax.broadcasted_iota(jnp.int32, (WIDE, TALL, size_z), 2) < 8
        for side in range(2):
            both = edge[side]
            both = both + turned(both, -32, 2)
            for c in range(3):
                part = jnp.where(inside, turned(both, -8 * c, 2), 0.0)
                grid[c, :, :, pl.ds(side * size_z, size_z)] += part

    def spread_rest(turn, polls):
        wait_round(turn)
        for side in range(2):
            for edge_plane in (0, WIDE - 1):
                edge[side, edge_plane] = jnp.zeros((TALL, size_z), jnp.float32)
        for step_x, step_y in FLAT:
            if step_x or step_y:
                spread_main(turn, step_x, step_y)
        for poll in polls:
            poll()
        for side in range(2):
            for step_x, step_y in FLAT:
                spread_side(turn, step_x, step_y, side)
        finish_sides()

    def add(value, axis):
        return turned(value, -1, axis) + turned(value, 1, axis)

    def sub(value, axis):
        return turned(value, -1, axis) - turned(value, 1, axis)

    def respond():
        scale = fields[3]
        mx, my, mz = (scale * grid[c] for c in range(3))
        slope_y, slope_z = sub(my, 1), sub(mz, 2)
        sum_x = 2.0 * mx + add(mx, 1) + add(mx, 2)
        slope = slope_y + slope_z
        px = sum_x[2:] + sum_x[:-2] + slope[2:] - slope[:-2]
        slope_x = mx[2:] - mx[:-2]
        sum_y = (2.0 * my + add(my, 2))[1:-1] + my[2:] + my[:-2]
        py = add(sum_y, 1) + sub(slope_x + slope_z[1:-1], 1)
        sum_z = (2.0 * mz + add(mz, 1))[1:-1] + mz[2:] + mz[:-2]
        pz = add(sum_z, 2) + sub(slope_x + slope_y[1:-1], 2)
        half = scale[1:-1] * 0.5
        return jnp.stack(
            [half * (m[1:-1] + p * (1.0 / 12.0)) for m, p in ((mx, px), (my, py), (mz, pz))]
        )

    def apply(turn, vector, polls=()):
        spread_rest(turn, polls)
        return live * (interpolate(respond()) + stiffness * vector)

    def partial_sums(residual, image):
        folded = []
        for other in (residual, image):
            line = jnp.sum(residual * other, axis=0, keepdims=True)
            total = line[:, :128]
            for at in range(128, cap, 128):
                total = total + line[:, at : at + 128]
            folded.append(total)
        return jnp.concatenate(folded, axis=0)

    def totals(tile):
        return (
            jnp.sum(tile[0:1], axis=1, keepdims=True),
            jnp.sum(tile[1:2], axis=1, keepdims=True),
        )

    loads[0].wait()
    loads[1].wait()
    pack()
    loads[2].wait()
    loads[3].wait()
    each = cap // 128
    for k, size in enumerate(sizes):
        local = (cells_ref[pl.ds(k, 1), :] - me[k] * size).astype(jnp.float32)
        for values, at in ((local, k), (offsets_ref[pl.ds(k, 1), :], k + 3)):
            for part in range(each):
                a, b = divmod(at * each + part, 4)
                nbuf[0, a, pl.ds(b, 1), :] = values[:, part * 128 : part * 128 + 128]
    for load in loads[4:]:
        load.wait()
    pl.semaphore_wait(barrier, len(peers))
    go(flows)
    go(edges)
    send_round(0)
    go(scalars)
    target, stiffness = target_ref[...], stiffness_ref[...]
    live = (lax.broadcasted_iota(jnp.int32, (1, cap), 1) < count_ref[0]).astype(jnp.float32)
    build_main(0, 0)
    edge[...] = jnp.zeros_like(edge)
    for copy in flows + edges:
        copy.wait_recv()
    widen((0, 1, 2), 0.0)
    base = live * (target - interpolate(fields[pl.ds(0, 3), pl.ds(1, own_planes)]))
    put(1, base)
    send_round(1)
    spread_main(1, 0, 0)
    wait_round(0)
    for step_x, step_y in FLAT:
        if step_x or step_y:
            build_main(step_x, step_y)
        build_side(step_x, step_y, 0)
        build_side(step_x, step_y, 1)
    for copy in scalars:
        copy.wait_recv()
    widen((3,), 1.0)
    first = apply(1, base)
    put(2, first)
    send_round(2)
    send_sum(0, 0, partial_sums(base, first))
    spread_main(2, 0, 0)
    second = apply(2, first, [lambda: send_sum(0, 1, wait_sum(0, 0))])
    put(3, second)
    send_round(3)
    spread_main(3, 0, 0)
    norm, product = totals(wait_sum(0, 1))
    alpha = norm / product
    answer = alpha * base
    residual, image = base - alpha * first, first - alpha * second
    send_sum(1, 0, partial_sums(residual, image))
    third = apply(3, second, [lambda: send_sum(1, 1, wait_sum(1, 0))])
    again = second - alpha * third
    norm_before, alpha_before = norm, alpha
    norm, product = totals(wait_sum(1, 1))
    ratio = norm / norm_before
    alpha = norm / (product - ratio * norm / alpha_before)
    direction = residual + ratio * base
    answer = answer + alpha * direction
    residual, image = (
        residual - alpha * (image + ratio * first),
        image - alpha * (again + ratio * second),
    )
    send_sum(2, 0, partial_sums(residual, image))
    send_sum(2, 1, wait_sum(2, 0))
    norm_before, alpha_before = norm, alpha
    norm, product = totals(wait_sum(2, 1))
    ratio = norm / norm_before
    alpha = norm / (product - ratio * norm / alpha_before)
    out[...] = answer + alpha * (residual + ratio * direction)
    for copy in sent:
        copy.wait_send()


def body(mesh_counts, density, base_velocity, cells, offsets, target, stiffness, counts):
    sizes = density.shape
    size_x, size_y, size_z = sizes
    cap = cells.shape[1]
    assert sizes == (8, 8, 128) and min(mesh_counts) > 2
    lanes = 2 * size_z
    number, flat = 27, 9
    turns = ITERS + 1
    near, far = mesh_counts[1] * mesh_counts[2], mesh_counts[0]
    halos = 34
    return pl.pallas_call(
        functools.partial(kernel, mesh_counts, sizes),
        out_shape=jax.ShapeDtypeStruct((3, cap), jnp.float32),
        in_specs=[pl.BlockSpec(memory_space=pltpu.HBM)] * 7,
        out_specs=pl.BlockSpec(memory_space=pltpu.VMEM),
        scratch_shapes=[
            pltpu.VMEM((4, size_x, size_y, size_z), jnp.float32),
            pltpu.VMEM((3, cap), jnp.int32),
            pltpu.VMEM((3, cap), jnp.float32),
            pltpu.VMEM((3, cap), jnp.float32),
            pltpu.VMEM((1, cap), jnp.float32),
            pltpu.SMEM((1,), jnp.int32),
            pltpu.VMEM((4, WIDE, TALL, lanes), jnp.float32),
            pltpu.VMEM((4, LOW + HIGH, size_y, size_z), jnp.float32),
            pltpu.VMEM((4, 2, size_y, size_z), jnp.float32),
            pltpu.VMEM((4, 4, size_y, size_z), jnp.float32),
            pltpu.VMEM((4, 4, size_y, size_z), jnp.float32),
            pltpu.VMEM((4, 7, size_y, size_z), jnp.float32),
            pltpu.VMEM((size_y, size_z), jnp.float32),
            pltpu.VMEM((size_y, size_z), jnp.float32),
            pltpu.VMEM((2, flat, size_y, size_z), jnp.float32),
            pltpu.VMEM((number, 3 * (cap // 256), 4, 128), jnp.float32),
            pltpu.VMEM((ITERS, number, 3 * (cap // 128), 128), jnp.float32),
            pltpu.VMEM((ITERS, near, 2, 128), jnp.float32),
            pltpu.VMEM((ITERS, far, 2, 128), jnp.float32),
            pltpu.VMEM((PATCH_ROWS, cap), jnp.float32),
            pltpu.VMEM((flat, lanes, cap), jnp.bfloat16),
            pltpu.VMEM((flat, lanes, cap), jnp.bfloat16),
            pltpu.VMEM((2, 2 * PATCH_ROWS, cap), jnp.bfloat16),
            pltpu.VMEM((2, flat, 8, cap), jnp.float32),
            pltpu.VMEM((2, WIDE, TALL, size_z), jnp.float32),
            pltpu.VMEM((3, WIDE, TALL, lanes), jnp.float32),
            pltpu.SemaphoreType.DMA((7,)),
            pltpu.SemaphoreType.DMA((turns, number - 1)),
            pltpu.SemaphoreType.DMA((turns, number - 1)),
            pltpu.SemaphoreType.DMA((ITERS, near - 1)),
            pltpu.SemaphoreType.DMA((ITERS, near - 1)),
            pltpu.SemaphoreType.DMA((ITERS, far - 1)),
            pltpu.SemaphoreType.DMA((ITERS, far - 1)),
            pltpu.SemaphoreType.DMA((halos,)),
            pltpu.SemaphoreType.DMA((halos,)),
        ],
        compiler_params=pltpu.CompilerParams(
            collective_id=0, has_side_effects=True, vmem_limit_bytes=60 * 1024 * 1024
        ),
    )(density, base_velocity, cells, offsets, target, stiffness[None], counts)


def solution(mesh):
    return jax.shard_map(
        functools.partial(body, tuple(mesh.shape[name] for name in AXES)),
        mesh=mesh,
        in_specs=(
            P("gx", "gy", "gz"),
            P(None, "gx", "gy", "gz"),
            P(None, ("gx", "gy", "gz")),
            P(None, ("gx", "gy", "gz")),
            P(None, ("gx", "gy", "gz")),
            P(("gx", "gy", "gz")),
            P(("gx", "gy", "gz")),
        ),
        out_specs=P(None, ("gx", "gy", "gz")),
        check_vma=False,
    )
```

time: 76.4 us -> 60.7 us (0.79)
  Pallas kernels: 74.3 us -> 58.7 us
    pallas_call x1, Pallas kernels: 74.3 us -> 58.7 us  [body(): pl.pallas_call(functools.partial(kernel, mesh_counts, sizes), out_shape=j...]
where the time goes in v2:
time: 60.7 us; the launch traced here: 60.6 us
  Pallas kernels  58.7 us (97%)
  local copies, waits for them, and re-layouts  1.28 us (2%)
  between operations  0.66 us (1%)
    pallas_call x1, Pallas kernels, body(): pl.pallas_call(functools.partial(kernel, mesh_counts, sizes), out_shape=j...  58.7 us
    unnamed x1, local copies, waits for them, and re-layouts  1.28 us

profile of v2, /device:TPU:1, one launch (start us, length us, event | category | flops | bytes accessed | tf_op | source)
XLA Modules:
  0.0 60.6 jit_solution(17590345119245448709)
XLA Ops:
  0.7 58.7 %shard_map.73 = f32[3,256]{1,0:T(4,128)} custom-call(f32[8,8,128]{2,1,0:T(8,128)} %density.1, f32[3,8,8,128]{3,2,1,0:T(8,128)} %velocity.1, s32[3,256]{1,0:T(4,128)} %cells_in.1, f32[3,256]{1,0:T(4,128)} %offsets_in.1, f32[3,256]{1,0:T(4,128)} %target_in.1, f32[1,256]{1,0:T(1,128)} %bitcast.1, s32[1]{0:T(128)S(6)} %copy.9.count_in), custom_call_target="tpu_custom_call" | custom-call | tf_op jit(solution)/shard_map/pallas_call | solution.py:543
  59.3 1.3 %copy.10 = f32[3,256]{1,0:T(4,128)} copy(f32[3,256]{1,0:T(4,128)} %shard_map.73) | data formatting | bytes 6144

commit v3 on v2

--- a/solution.py
+++ b/solution.py
@@ -115,14 +115,25 @@
     def go(copies):
         for copy in copies:
             copy.start()
-            sent.append(copy)
+
+    def every(ref, send, receive):
+        copy = pltpu.make_async_remote_copy(
+            src_ref=ref,
+            dst_ref=ref,
+            send_sem=send,
+            recv_sem=receive,
+            device_id=device(far[0]),
+            device_id_type=MESH_ID,
+        )
+        sent.append(copy)
+        return copy
 
     def neighbour_copy(turn, number):
         return pltpu.make_async_remote_copy(
             src_ref=fbuf.at[turn - 1, 0] if turn else nbuf.at[0],
             dst_ref=fbuf.at[turn - 1, number] if turn else nbuf.at[number],
-            send_sem=nsend.at[turn, number - 1],
-            recv_sem=nrecv.at[turn, number - 1],
+            send_sem=nsend.at[turn],
+            recv_sem=nrecv.at[turn],
             device_id=device(negated(slots[number])),
             device_id_type=MESH_ID,
         )
@@ -132,16 +143,17 @@
         go([neighbour_copy(turn, number) for number in far_first])
 
     def wait_round(turn):
-        for number in range(1, len(slots)):
-            neighbour_copy(turn, number).wait_recv()
+        others = pl.ds(1, len(slots) - 1)
+        landed = fbuf.at[turn - 1, others] if turn else nbuf.at[others]
+        every(landed, nsend.at[turn], nrecv.at[turn]).wait_recv()
 
     def sum_copy(turn, stage, number):
         members, buffer, send, receive = ((near, rbuf, rsend, rrecv), (far, sbuf, ssend, srecv))[stage]
         return pltpu.make_async_remote_copy(
             src_ref=buffer.at[turn, 0],
             dst_ref=buffer.at[turn, number + 1],
-            send_sem=send.at[turn, number],
-            recv_sem=receive.at[turn, number],
+            send_sem=send.at[turn],
+            recv_sem=receive.at[turn],
             device_id=device(negated(members[number])),
             device_id_type=MESH_ID,
         )
@@ -156,22 +168,20 @@
         go([sum_copy(turn, stage, number) for number in ordered])
 
     def wait_sum(turn, stage):
-        members, buffer = ((near, rbuf), (far, sbuf))[stage]
-        for number in sorted(range(len(members)), key=lambda k: (-away(members[k]), k)):
-            sum_copy(turn, stage, number).wait_recv()
+        members, buffer, send, receive = ((near, rbuf, rsend, rrecv), (far, sbuf, ssend, srecv))[stage]
+        every(buffer.at[turn, pl.ds(1, len(members))], send.at[turn], receive.at[turn]).wait_recv()
         return jnp.sum(buffer[turn], axis=0)
 
     def put(turn, vector):
         for c in range(3):
             for part in range(cap // 128):
-                fbuf[turn - 1, 0, pl.ds(c * (cap // 128) + part, 1), :] = vector[
+                fbuf[turn - 1, 0, c, pl.ds(part, 1), :] = vector[
                     c : c + 1, part * 128 : part * 128 + 128
                 ]
 
     def joined(ref, at, number, k):
-        each = cap // 128
         return jnp.concatenate(
-            [ref[at, number, pl.ds(k * each + part, 1), :] for part in range(each)], axis=1
+            [ref[at, number, k, pl.ds(part, 1), :] for part in range(cap // 128)], axis=1
         )
 
     def mark(number, k):
@@ -189,40 +199,45 @@
             device_id_type=MESH_ID,
         )
 
-    flows, scalars = [], []
+    flows, scalars, edges = [], [], []
     plane_of = {-1: (size_x - LOW, LOW, 0), 1: (0, HIGH, LOW)}
     low_of = {-1: (1, 1, 0), 0: (0, 2, 1), 1: (0, 1, 3)}
     high_of = {-1: (3, 1, 0), 0: (0, 4, 1), 1: (0, 2, 5)}
-    for copies, part in ((flows, pl.ds(0, 3)), (scalars, pl.ds(3, 1))):
-        for step_x, step_y in sorted(FLAT, key=lambda o: -abs(o[0]) - abs(o[1])):
-            if step_y:
-                source, target, where = (
-                    (ylow, below, low_of) if step_y < 0 else (yhigh, above, high_of)
-                )
-            elif step_x:
-                source, target, where = block, xbuf, plane_of
-            else:
+    spaces = ((block, xbuf, plane_of), (ylow, below, low_of), (yhigh, above, high_of))
+    corners_first = sorted(FLAT, key=lambda o: -abs(o[0]) - abs(o[1]))
+    halves = (pl.ds(0, 3), pl.ds(3, 1))
+    for kind, copies in enumerate((flows, scalars)):
+        for step_x, step_y in corners_first:
+            if step_x == step_y == 0:
                 continue
+            space = 0 if step_y == 0 else 1 if step_y < 0 else 2
+            source, target, where = spaces[space]
             first, many, at = where[step_x]
             copies.append(
                 halo_copy(
-                    len(flows) + len(scalars),
-                    source.at[part, pl.ds(first, many)],
-                    target.at[part, pl.ds(at, many)],
+                    3 * kind + space,
+                    source.at[halves[kind], pl.ds(first, many)],
+                    target.at[halves[kind], pl.ds(at, many)],
                     (step_x, step_y, 0),
                 )
             )
-    edges = []
-    for k, (step_x, step_y) in sorted(enumerate(FLAT), key=lambda o: -abs(o[1][0]) - abs(o[1][1])):
+    for step_x, step_y in corners_first:
         for side, step_z in enumerate((-1, 1)):
             edges.append(
                 halo_copy(
-                    len(flows) + len(scalars) + len(edges),
+                    6,
                     (zlow, zhigh)[side],
-                    zbuf.at[side, k],
+                    zbuf.at[side, FLAT.index((step_x, step_y))],
                     (step_x, step_y, step_z),
                 )
             )
+
+    def wait_halos(kind):
+        for space, (_, target, _) in enumerate(spaces):
+            at = 3 * kind + space
+            every(target.at[halves[kind]], hsend.at[at], hrecv.at[at]).wait_recv()
+        if kind == 0:
+            every(zbuf, hsend.at[6], hrecv.at[6]).wait_recv()
 
     lane = lax.broadcasted_iota(jnp.int32, (size_y, size_z), 1)
     row = lax.broadcasted_iota(jnp.int32, (size_y, size_z), 0)
@@ -396,16 +411,18 @@
                 part = jnp.where(inside, turned(both, -8 * c, 2), 0.0)
                 grid[c, :, :, pl.ds(side * size_z, size_z)] += part
 
-    def spread_rest(turn, polls):
+    def spread_rest(turn, early, late):
         wait_round(turn)
+        if early:
+            early()
         for side in range(2):
             for edge_plane in (0, WIDE - 1):
                 edge[side, edge_plane] = jnp.zeros((TALL, size_z), jnp.float32)
         for step_x, step_y in FLAT:
             if step_x or step_y:
                 spread_main(turn, step_x, step_y)
-        for poll in polls:
-            poll()
+        if late:
+            late()
         for side in range(2):
             for step_x, step_y in FLAT:
                 spread_side(turn, step_x, step_y, side)
@@ -434,8 +451,8 @@
             [half * (m[1:-1] + p * (1.0 / 12.0)) for m, p in ((mx, px), (my, py), (mz, pz))]
         )
 
-    def apply(turn, vector, polls=()):
-        spread_rest(turn, polls)
+    def apply(turn, vector, early=None, late=None):
+        spread_rest(turn, early, late)
         return live * (interpolate(respond()) + stiffness * vector)
 
     def partial_sums(residual, image):
@@ -477,8 +494,7 @@
     live = (lax.broadcasted_iota(jnp.int32, (1, cap), 1) < count_ref[0]).astype(jnp.float32)
     build_main(0, 0)
     edge[...] = jnp.zeros_like(edge)
-    for copy in flows + edges:
-        copy.wait_recv()
+    wait_halos(0)
     widen((0, 1, 2), 0.0)
     base = live * (target - interpolate(fields[pl.ds(0, 3), pl.ds(1, own_planes)]))
     put(1, base)
@@ -490,15 +506,14 @@
             build_main(step_x, step_y)
         build_side(step_x, step_y, 0)
         build_side(step_x, step_y, 1)
-    for copy in scalars:
-        copy.wait_recv()
+    wait_halos(1)
     widen((3,), 1.0)
     first = apply(1, base)
     put(2, first)
     send_round(2)
     send_sum(0, 0, partial_sums(base, first))
     spread_main(2, 0, 0)
-    second = apply(2, first, [lambda: send_sum(0, 1, wait_sum(0, 0))])
+    second = apply(2, first, early=lambda: send_sum(0, 1, wait_sum(0, 0)))
     put(3, second)
     send_round(3)
     spread_main(3, 0, 0)
@@ -507,7 +522,7 @@
     answer = alpha * base
     residual, image = base - alpha * first, first - alpha * second
     send_sum(1, 0, partial_sums(residual, image))
-    third = apply(3, second, [lambda: send_sum(1, 1, wait_sum(1, 0))])
+    third = apply(3, second, late=lambda: send_sum(1, 1, wait_sum(1, 0)))
     again = second - alpha * third
     norm_before, alpha_before = norm, alpha
     norm, product = totals(wait_sum(1, 1))
@@ -539,7 +554,6 @@
     number, flat = 27, 9
     turns = ITERS + 1
     near, far = mesh_counts[1] * mesh_counts[2], mesh_counts[0]
-    halos = 34
     return pl.pallas_call(
         functools.partial(kernel, mesh_counts, sizes),
         out_shape=jax.ShapeDtypeStruct((3, cap), jnp.float32),
@@ -562,7 +576,7 @@
             pltpu.VMEM((size_y, size_z), jnp.float32),
             pltpu.VMEM((2, flat, size_y, size_z), jnp.float32),
             pltpu.VMEM((number, 3 * (cap // 256), 4, 128), jnp.float32),
-            pltpu.VMEM((ITERS, number, 3 * (cap // 128), 128), jnp.float32),
+            pltpu.VMEM((ITERS, number, 3, cap // 128, 128), jnp.float32),
             pltpu.VMEM((ITERS, near, 2, 128), jnp.float32),
             pltpu.VMEM((ITERS, far, 2, 128), jnp.float32),
             pltpu.VMEM((PATCH_ROWS, cap), jnp.float32),
@@ -573,14 +587,14 @@
             pltpu.VMEM((2, WIDE, TALL, size_z), jnp.float32),
             pltpu.VMEM((3, WIDE, TALL, lanes), jnp.float32),
             pltpu.SemaphoreType.DMA((7,)),
-            pltpu.SemaphoreType.DMA((turns, number - 1)),
-            pltpu.SemaphoreType.DMA((turns, number - 1)),
-            pltpu.SemaphoreType.DMA((ITERS, near - 1)),
-            pltpu.SemaphoreType.DMA((ITERS, near - 1)),
-            pltpu.SemaphoreType.DMA((ITERS, far - 1)),
-            pltpu.SemaphoreType.DMA((ITERS, far - 1)),
-            pltpu.SemaphoreType.DMA((halos,)),
-            pltpu.SemaphoreType.DMA((halos,)),
+            pltpu.SemaphoreType.DMA((turns,)),
+            pltpu.SemaphoreType.DMA((turns,)),
+            pltpu.SemaphoreType.DMA((ITERS,)),
+            pltpu.SemaphoreType.DMA((ITERS,)),
+            pltpu.SemaphoreType.DMA((ITERS,)),
+            pltpu.SemaphoreType.DMA((ITERS,)),
+            pltpu.SemaphoreType.DMA((7,)),
+            pltpu.SemaphoreType.DMA((7,)),
         ],
         compiler_params=pltpu.CompilerParams(
             collective_id=0, has_side_effects=True, vmem_limit_bytes=60 * 1024 * 1024

time: 60.7 us -> 55.3 us (0.911)
  Pallas kernels: 58.7 us -> 53.2 us
    pallas_call x1, Pallas kernels: 58.7 us -> 53.2 us  [body(): pl.pallas_call(functools.partial(kernel, mesh_counts, sizes), out_shape=j...]
where the time goes in v3:
time: 55.3 us; the launch traced here: 55.2 us
  Pallas kernels  53.2 us (96%)
  local copies, waits for them, and re-layouts  1.28 us (2%)
  between operations  0.66 us (1%)
    pallas_call x1, Pallas kernels, body(): pl.pallas_call(functools.partial(kernel, mesh_counts, sizes), out_shape=j...  53.2 us
    unnamed x1, local copies, waits for them, and re-layouts  1.28 us

profile of v3, /device:TPU:1, one launch (start us, length us, event | category | flops | bytes accessed | tf_op | source)
XLA Modules:
  0.0 55.2 jit_solution(922474785109252844)
XLA Ops:
  0.7 53.2 %shard_map.73 = f32[3,256]{1,0:T(4,128)} custom-call(f32[8,8,128]{2,1,0:T(8,128)} %density.1, f32[3,8,8,128]{3,2,1,0:T(8,128)} %velocity.1, s32[3,256]{1,0:T(4,128)} %cells_in.1, f32[3,256]{1,0:T(4,128)} %offsets_in.1, f32[3,256]{1,0:T(4,128)} %target_in.1, f32[1,256]{1,0:T(1,128)} %bitcast.1, s32[1]{0:T(128)S(6)} %copy.9.count_in), custom_call_target="tpu_custom_call" | custom-call | tf_op jit(solution)/shard_map/pallas_call | solution.py:557
  53.9 1.3 %copy.10 = f32[3,256]{1,0:T(4,128)} copy(f32[3,256]{1,0:T(4,128)} %shard_map.73) | data formatting | bytes 6144

commit v4 on v3

--- a/solution.py
+++ b/solution.py
@@ -71,9 +71,9 @@
 def kernel(
     counts, sizes, density, velocity, cells_in, offsets_in, target_in, stiffness_in, count_in, out,
     block, cells_ref, offsets_ref, target_ref, stiffness_ref, count_ref,
-    fields, xbuf, ylow, yhigh, below, above, zlow, zhigh, zbuf, nbuf, fbuf, rbuf, sbuf,
+    fields, xbuf, ylow, yhigh, below, above, zlow, zhigh, zbuf, nbuf, fbuf, rbuf, sbuf, dbuf,
     txy, thi, tlo, azz, tzz, edge, grid,
-    lsem, nsend, nrecv, rsend, rrecv, ssend, srecv, hsend, hrecv,
+    lsem, nsend, nrecv, ssend, srecv, hsend, hrecv,
 ):
     size_x, size_y, size_z = sizes
     cap = cells_ref.shape[1]
@@ -90,6 +90,7 @@
 
     near = [o for o in itertools.product([0], range(counts[1]), range(counts[2])) if any(o)]
     far = [(o, 0, 0) for o in range(1, counts[0])]
+    whole = [o for o in itertools.product(*[range(n) for n in counts]) if any(o)]
     wrapped = {tuple(o % n for o, n in zip(slot, counts)) for slot in slots if any(slot)}
     peers = sorted(wrapped | set(near) | set(far))
     loads = [
@@ -147,30 +148,37 @@
         landed = fbuf.at[turn - 1, others] if turn else nbuf.at[others]
         every(landed, nsend.at[turn], nrecv.at[turn]).wait_recv()
 
-    def sum_copy(turn, stage, number):
-        members, buffer, send, receive = ((near, rbuf, rsend, rrecv), (far, sbuf, ssend, srecv))[stage]
-        return pltpu.make_async_remote_copy(
-            src_ref=buffer.at[turn, 0],
-            dst_ref=buffer.at[turn, number + 1],
-            send_sem=send.at[turn],
-            recv_sem=receive.at[turn],
-            device_id=device(negated(members[number])),
-            device_id_type=MESH_ID,
-        )
-
     def away(offset):
-        return -sum(min(o, n - o) for o, n in zip(offset, counts))
-
-    def send_sum(turn, stage, value):
-        members, buffer = ((near, rbuf), (far, sbuf))[stage]
-        buffer[turn, 0] = value
-        ordered = sorted(range(len(members)), key=lambda k: (away(members[k]), k))
-        go([sum_copy(turn, stage, number) for number in ordered])
-
-    def wait_sum(turn, stage):
-        members, buffer, send, receive = ((near, rbuf, rsend, rrecv), (far, sbuf, ssend, srecv))[stage]
-        every(buffer.at[turn, pl.ds(1, len(members))], send.at[turn], receive.at[turn]).wait_recv()
-        return jnp.sum(buffer[turn], axis=0)
+        return sum(min(o, n - o) for o, n in zip(offset, counts))
+
+    stages = {
+        "near": (near, rbuf.at[0], ssend.at[0], srecv.at[0]),
+        "far": (far, sbuf.at[0], ssend.at[1], srecv.at[1]),
+        1: (whole, dbuf.at[0], ssend.at[2], srecv.at[2]),
+        2: (whole, dbuf.at[1], ssend.at[3], srecv.at[3]),
+    }
+
+    def send_sum(stage, value):
+        members, buffer, send, receive = stages[stage]
+        buffer[0] = value
+        for number in sorted(range(len(members)), key=lambda k: (-away(members[k]), k)):
+            pltpu.make_async_remote_copy(
+                src_ref=buffer.at[0],
+                dst_ref=buffer.at[number + 1],
+                send_sem=send,
+                recv_sem=receive,
+                device_id=device(negated(members[number])),
+                device_id_type=MESH_ID,
+            ).start()
+
+    def wait_sum(stage):
+        members, buffer, send, receive = stages[stage]
+        every(buffer.at[pl.ds(1, len(members))], send, receive).wait_recv()
+        total = buffer[...]
+        while total.shape[0] > 1:
+            half = total.shape[0] // 2
+            total = total[:half] + total[half:]
+        return total[0]
 
     def put(turn, vector):
         for c in range(3):
@@ -411,18 +419,14 @@
                 part = jnp.where(inside, turned(both, -8 * c, 2), 0.0)
                 grid[c, :, :, pl.ds(side * size_z, size_z)] += part
 
-    def spread_rest(turn, early, late):
+    def spread_rest(turn):
         wait_round(turn)
-        if early:
-            early()
         for side in range(2):
             for edge_plane in (0, WIDE - 1):
                 edge[side, edge_plane] = jnp.zeros((TALL, size_z), jnp.float32)
         for step_x, step_y in FLAT:
             if step_x or step_y:
                 spread_main(turn, step_x, step_y)
-        if late:
-            late()
         for side in range(2):
             for step_x, step_y in FLAT:
                 spread_side(turn, step_x, step_y, side)
@@ -451,9 +455,11 @@
             [half * (m[1:-1] + p * (1.0 / 12.0)) for m, p in ((mx, px), (my, py), (mz, pz))]
         )
 
-    def apply(turn, vector, early=None, late=None):
-        spread_rest(turn, early, late)
+    def apply(turn, vector):
+        spread_rest(turn)
         return live * (interpolate(respond()) + stiffness * vector)
+
+    left_half = lax.broadcasted_iota(jnp.int32, (1, 128), 1) < 64
 
     def partial_sums(residual, image):
         folded = []
@@ -462,13 +468,13 @@
             total = line[:, :128]
             for at in range(128, cap, 128):
                 total = total + line[:, at : at + 128]
-            folded.append(total)
-        return jnp.concatenate(folded, axis=0)
+            folded.append(total + turned(total, 64, 1))
+        return jnp.where(left_half, folded[0], folded[1])
 
     def totals(tile):
         return (
-            jnp.sum(tile[0:1], axis=1, keepdims=True),
-            jnp.sum(tile[1:2], axis=1, keepdims=True),
+            jnp.sum(jnp.where(left_half, tile, 0.0), axis=1, keepdims=True),
+            jnp.sum(jnp.where(left_half, 0.0, tile), axis=1, keepdims=True),
         )
 
     loads[0].wait()
@@ -509,23 +515,24 @@
     wait_halos(1)
     widen((3,), 1.0)
     first = apply(1, base)
+    send_sum("near", partial_sums(base, first))
     put(2, first)
     send_round(2)
-    send_sum(0, 0, partial_sums(base, first))
     spread_main(2, 0, 0)
-    second = apply(2, first, early=lambda: send_sum(0, 1, wait_sum(0, 0)))
+    send_sum("far", wait_sum("near"))
+    second = apply(2, first)
     put(3, second)
     send_round(3)
     spread_main(3, 0, 0)
-    norm, product = totals(wait_sum(0, 1))
+    norm, product = totals(wait_sum("far"))
     alpha = norm / product
     answer = alpha * base
     residual, image = base - alpha * first, first - alpha * second
-    send_sum(1, 0, partial_sums(residual, image))
-    third = apply(3, second, late=lambda: send_sum(1, 1, wait_sum(1, 0)))
+    send_sum(1, partial_sums(residual, image))
+    third = apply(3, second)
     again = second - alpha * third
     norm_before, alpha_before = norm, alpha
-    norm, product = totals(wait_sum(1, 1))
+    norm, product = totals(wait_sum(1))
     ratio = norm / norm_before
     alpha = norm / (product - ratio * norm / alpha_before)
     direction = residual + ratio * base
@@ -534,10 +541,9 @@
         residual - alpha * (image + ratio * first),
         image - alpha * (again + ratio * second),
     )
-    send_sum(2, 0, partial_sums(residual, image))
-    send_sum(2, 1, wait_sum(2, 0))
+    send_sum(2, partial_sums(residual, image))
     norm_before, alpha_before = norm, alpha
-    norm, product = totals(wait_sum(2, 1))
+    norm, product = totals(wait_sum(2))
     ratio = norm / norm_before
     alpha = norm / (product - ratio * norm / alpha_before)
     out[...] = answer + alpha * (residual + ratio * direction)
@@ -577,8 +583,9 @@
             pltpu.VMEM((2, flat, size_y, size_z), jnp.float32),
             pltpu.VMEM((number, 3 * (cap // 256), 4, 128), jnp.float32),
             pltpu.VMEM((ITERS, number, 3, cap // 128, 128), jnp.float32),
-            pltpu.VMEM((ITERS, near, 2, 128), jnp.float32),
-            pltpu.VMEM((ITERS, far, 2, 128), jnp.float32),
+            pltpu.VMEM((1, near, 1, 128), jnp.float32),
+            pltpu.VMEM((1, far, 1, 128), jnp.float32),
+            pltpu.VMEM((2, near * far, 1, 128), jnp.float32),
             pltpu.VMEM((PATCH_ROWS, cap), jnp.float32),
             pltpu.VMEM((flat, lanes, cap), jnp.bfloat16),
             pltpu.VMEM((flat, lanes, cap), jnp.bfloat16),
@@ -589,10 +596,8 @@
             pltpu.SemaphoreType.DMA((7,)),
             pltpu.SemaphoreType.DMA((turns,)),
             pltpu.SemaphoreType.DMA((turns,)),
-            pltpu.SemaphoreType.DMA((ITERS,)),
-            pltpu.SemaphoreType.DMA((ITERS,)),
-            pltpu.SemaphoreType.DMA((ITERS,)),
-            pltpu.SemaphoreType.DMA((ITERS,)),
+            pltpu.SemaphoreType.DMA((4,)),
+            pltpu.SemaphoreType.DMA((4,)),
             pltpu.SemaphoreType.DMA((7,)),
             pltpu.SemaphoreType.DMA((7,)),
         ],

time: 55.3 us -> 52 us (0.940)
  Pallas kernels: 53.2 us -> 49.9 us
    pallas_call x1, Pallas kernels: 53.2 us -> 49.9 us  [body(): pl.pallas_call(functools.partial(kernel, mesh_counts, sizes), out_shape=j...]
where the time goes in v4:
time: 52 us; the launch traced here: 51.9 us
  Pallas kernels  49.9 us (96%)
  local copies, waits for them, and re-layouts  1.28 us (2%)
  between operations  0.66 us (1%)
    pallas_call x1, Pallas kernels, body(): pl.pallas_call(functools.partial(kernel, mesh_counts, sizes), out_shape=j...  49.9 us
    unnamed x1, local copies, waits for them, and re-layouts  1.28 us

profile of v4, /device:TPU:1, one launch (start us, length us, event | category | flops | bytes accessed | tf_op | source)
XLA Modules:
  0.0 51.9 jit_solution(15624019642590703437)
XLA Ops:
  0.7 49.9 %shard_map.73 = f32[3,256]{1,0:T(4,128)} custom-call(f32[8,8,128]{2,1,0:T(8,128)} %density.1, f32[3,8,8,128]{3,2,1,0:T(8,128)} %velocity.1, s32[3,256]{1,0:T(4,128)} %cells_in.1, f32[3,256]{1,0:T(4,128)} %offsets_in.1, f32[3,256]{1,0:T(4,128)} %target_in.1, f32[1,256]{1,0:T(1,128)} %bitcast.1, s32[1]{0:T(128)S(6)} %copy.9.count_in), custom_call_target="tpu_custom_call" | custom-call | tf_op jit(solution)/shard_map/pallas_call | solution.py:563
  50.6 1.3 %copy.10 = f32[3,256]{1,0:T(4,128)} copy(f32[3,256]{1,0:T(4,128)} %shard_map.73) | data formatting | bytes 6144

commit v5 on v4

--- a/solution.py
+++ b/solution.py
@@ -9,7 +9,8 @@
 from jax.sharding import PartitionSpec as P
 
 ITERS = 3
-LOW, HIGH = 2, 3
+LOW = 2
+KINDS = (((0, 1, 2), 1, 2, 2), ((3,), 2, 3, 4))
 WIDE, TALL, HALF = 13, 16, 8
 STEPS = (0, -1, 1)
 MESH_ID = pl.DeviceIdType.MESH
@@ -71,7 +72,8 @@
 def kernel(
     counts, sizes, density, velocity, cells_in, offsets_in, target_in, stiffness_in, count_in, out,
     block, cells_ref, offsets_ref, target_ref, stiffness_ref, count_ref,
-    fields, xbuf, ylow, yhigh, below, above, zlow, zhigh, zbuf, nbuf, fbuf, rbuf, sbuf, dbuf,
+    fields, low_v, high_v, start_v, end_v, x_v, below_v, above_v, z_v,
+    low_d, high_d, start_d, end_d, x_d, below_d, above_d, z_d, nbuf, fbuf, rbuf, sbuf, dbuf,
     txy, thi, tlo, azz, tzz, edge, grid,
     lsem, nsend, nrecv, ssend, srecv, hsend, hrecv,
 ):
@@ -81,6 +83,8 @@
     slots = list(itertools.product(STEPS, STEPS, STEPS))
     me = [lax.axis_index(name) for name in AXES]
     sent = []
+    packs = ((low_v, high_v, start_v, end_v), (low_d, high_d, start_d, end_d))
+    landing = ((x_v, below_v, above_v, z_v), (x_d, below_d, above_d, z_d))
 
     def device(offset):
         return tuple(lax.rem(m + (o % n), n) for m, o, n in zip(me, offset, counts))
@@ -92,7 +96,8 @@
     far = [(o, 0, 0) for o in range(1, counts[0])]
     whole = [o for o in itertools.product(*[range(n) for n in counts]) if any(o)]
     wrapped = {tuple(o % n for o, n in zip(slot, counts)) for slot in slots if any(slot)}
-    peers = sorted(wrapped | set(near) | set(far))
+    half_way = {(counts[0] // 2, 0, 0), (0, counts[1] // 2, 0)}
+    peers = sorted(wrapped | half_way)
     loads = [
         pltpu.make_async_copy(source, destination, lsem.at[k])
         for k, (source, destination) in enumerate(
@@ -107,11 +112,11 @@
             ]
         )
     ]
-    for load in loads:
-        load.start()
     barrier = pltpu.get_barrier_semaphore()
     for peer in peers:
         pl.semaphore_signal(barrier, inc=1, device_id=device(peer), device_id_type=MESH_ID)
+    for load in loads:
+        load.start()
 
     def go(copies):
         for copy in copies:
@@ -207,45 +212,50 @@
             device_id_type=MESH_ID,
         )
 
-    flows, scalars, edges = [], [], []
-    plane_of = {-1: (size_x - LOW, LOW, 0), 1: (0, HIGH, LOW)}
-    low_of = {-1: (1, 1, 0), 0: (0, 2, 1), 1: (0, 1, 3)}
-    high_of = {-1: (3, 1, 0), 0: (0, 4, 1), 1: (0, 2, 5)}
-    spaces = ((block, xbuf, plane_of), (ylow, below, low_of), (yhigh, above, high_of))
     corners_first = sorted(FLAT, key=lambda o: -abs(o[0]) - abs(o[1]))
-    halves = (pl.ds(0, 3), pl.ds(3, 1))
-    for kind, copies in enumerate((flows, scalars)):
+
+    def halos(kind):
+        parts, low, high, slot = KINDS[kind]
+        (source_x, source_low, source_high, source_start, source_end), targets = (
+            (block.at[pl.ds(parts[0], len(parts))], *packs[kind]),
+            landing[kind],
+        )
+        more = -(-high * slot // size_y)
+        spaces = (
+            (source_x, targets[0], {-1: (size_x - low, low, 0), 1: (0, high, low)}),
+            (source_low, targets[1], {-1: (low - 1, 1, 0), 0: (0, low, 1), 1: (0, 1, low + 1)}),
+            (source_high, targets[2], {-1: (slot - 1, 1, 0), 0: (0, slot, 1), 1: (0, more, slot + 1)}),
+        )
+        copies = []
         for step_x, step_y in corners_first:
-            if step_x == step_y == 0:
-                continue
-            space = 0 if step_y == 0 else 1 if step_y < 0 else 2
-            source, target, where = spaces[space]
-            first, many, at = where[step_x]
-            copies.append(
-                halo_copy(
-                    3 * kind + space,
-                    source.at[halves[kind], pl.ds(first, many)],
-                    target.at[halves[kind], pl.ds(at, many)],
-                    (step_x, step_y, 0),
+            if step_x or step_y:
+                space = 0 if step_y == 0 else 1 if step_y < 0 else 2
+                source, target, where = spaces[space]
+                first, many, at = where[step_x]
+                copies.append(
+                    halo_copy(
+                        4 * kind + space,
+                        source.at[:, pl.ds(first, many)],
+                        target.at[:, pl.ds(at, many)],
+                        (step_x, step_y, 0),
+                    )
                 )
-            )
-    for step_x, step_y in corners_first:
-        for side, step_z in enumerate((-1, 1)):
-            edges.append(
-                halo_copy(
-                    6,
-                    (zlow, zhigh)[side],
-                    zbuf.at[side, FLAT.index((step_x, step_y))],
-                    (step_x, step_y, step_z),
+        for step_x, step_y in corners_first:
+            for side, step_z in enumerate((-1, 1)):
+                copies.append(
+                    halo_copy(
+                        4 * kind + 3,
+                        (source_start, source_end)[side],
+                        targets[3].at[side, FLAT.index((step_x, step_y))],
+                        (step_x, step_y, step_z),
+                    )
                 )
-            )
+        return copies
 
     def wait_halos(kind):
-        for space, (_, target, _) in enumerate(spaces):
-            at = 3 * kind + space
-            every(target.at[halves[kind]], hsend.at[at], hrecv.at[at]).wait_recv()
-        if kind == 0:
-            every(zbuf, hsend.at[6], hrecv.at[6]).wait_recv()
+        for space, target in enumerate(landing[kind]):
+            at = 4 * kind + space
+            every(target, hsend.at[at], hrecv.at[at]).wait_recv()
 
     lane = lax.broadcasted_iota(jnp.int32, (size_y, size_z), 1)
     row = lax.broadcasted_iota(jnp.int32, (size_y, size_z), 0)
@@ -254,75 +264,78 @@
         by %= value.shape[axis]
         return pltpu.roll(value, by, axis) if by else value
 
-    def pack():
-        low = [jnp.zeros((size_y, size_z), jnp.float32)] * 2
-        high = [jnp.zeros((size_y, size_z), jnp.float32)] * 2
-        for c in range(4):
-            tiles_low = [None] * 2
-            tiles_high = [None] * 4
+    def pack(kind):
+        parts, low, high, slot = KINDS[kind]
+        source_low, source_high, source_start, source_end = packs[kind]
+        starts = [jnp.zeros((size_y, size_z), jnp.float32)] * 2
+        ends = [jnp.zeros((size_y, size_z), jnp.float32)] * 2
+        for i, c in enumerate(parts):
+            tiles_low, tiles_high = [None] * low, [None] * slot
             for plane in range(size_x):
                 own = block[c, plane]
-                t, q = divmod(plane, 4)
-                moved = turned(own, 2 * q - 6, 0)
-                tiles_low[t] = moved if q == 0 else jnp.where(row // 2 == q, moved, tiles_low[t])
-                t, q = divmod(plane, 2)
-                moved = turned(own, 4 * q, 0)
-                tiles_high[t] = moved if q == 0 else jnp.where(row // 4 == q, moved, tiles_high[t])
-                at = c * size_x + plane
+                t, q = divmod(plane, size_y // low)
+                moved = turned(own, low * (q + 1) - size_y, 0)
+                tiles_low[t] = moved if q == 0 else jnp.where(row // low == q, moved, tiles_low[t])
+                t, q = divmod(plane, size_y // slot)
+                moved = turned(own, slot * q, 0)
+                tiles_high[t] = moved if q == 0 else jnp.where(row // slot == q, moved, tiles_high[t])
+                at = i * size_x + plane
                 chain = plane % 2
-                low[chain] = jnp.where(
-                    lane // 2 == at, turned(own, 2 * at - (size_z - LOW), 1), low[chain]
+                starts[chain] = jnp.where(
+                    lane // low == at, turned(own, low * (at + 1) - size_z, 1), starts[chain]
                 )
-                high[chain] = jnp.where(lane // 4 == at, turned(own, 4 * at, 1), high[chain])
-            for t in range(2):
-                ylow[c, t] = tiles_low[t]
-            for t in range(4):
-                yhigh[c, t] = tiles_high[t]
-        zlow[...] = jnp.where(lane // 2 % 2 == 0, low[0], low[1])
-        zhigh[...] = jnp.where(lane // 4 % 2 == 0, high[0], high[1])
+                ends[chain] = jnp.where(lane // slot == at, turned(own, slot * at, 1), ends[chain])
+            for t in range(low):
+                source_low[i, t] = tiles_low[t]
+            for t in range(slot):
+                source_high[i, t] = tiles_high[t]
+        source_start[...] = jnp.where(lane // low % 2 == 0, starts[0], starts[1])
+        source_end[...] = jnp.where(lane // slot % 2 == 0, ends[0], ends[1])
 
     def tall_of(down, own, up):
         moved = turned(own, LOW, 0)
-        return (
-            jnp.where(row < LOW, down, moved),
-            jnp.where(row < LOW, moved, up),
-        )
-
-    def widen(components, first):
+        return jnp.where(row < LOW, down, moved), jnp.where(row < LOW, moved, up)
+
+    def widen(kind):
+        parts, low, high, slot = KINDS[kind]
+        xbuf, below, above, zbuf = landing[kind]
+        blank = 1.0 if kind else 0.0
         sides = {}
         for step_x in STEPS:
             for side in range(2):
                 down, own, up = (zbuf[side, FLAT.index((step_x, step_y))] for step_y in (-1, 0, 1))
                 sides[step_x, side] = tall_of(turned(down, LOW, 0), own, turned(up, LOW, 0))
-        for plane in range(WIDE):
-            if plane < LOW:
-                step_x, x = -1, plane + size_x - LOW
-            elif plane < LOW + size_x:
-                step_x, x = 0, plane - LOW
-            else:
-                step_x, x = 1, plane - LOW - size_x
-            for c in components:
-                own = block[c, x] if step_x == 0 else xbuf[c, plane if step_x < 0 else plane - size_x]
-                source, _, at = low_of[step_x]
-                down = turned(below[c, at + x // 4 - source], -2 * (x % 4), 0)
-                source, _, at = high_of[step_x]
-                up = turned(above[c, at + x // 2 - source], LOW - 4 * (x % 2), 0)
-                talls = tall_of(down, own, up)
-                index = c * size_x + x
+        for x in range(-low, size_x + high):
+            step_x = -1 if x < 0 else 0 if x < size_x else 1
+            inner = x - step_x * size_x
+            for i, c in enumerate(parts):
+                own = block[c, x] if step_x == 0 else xbuf[i, x + low if step_x < 0 else x - size_x + low]
+                t, q = divmod(inner, size_y // low)
+                t = (0, t + 1, low + 1)[step_x + 1]
+                down = turned(below[i, t], LOW - low * (q + 1), 0)
+                t, q = divmod(inner, size_y // slot)
+                t = (0, t + 1, t + slot + 1)[step_x + 1]
+                up = turned(above[i, t], LOW - slot * q, 0)
+                if low < LOW:
+                    down = jnp.where(row >= LOW - low, down, blank)
+                talls = tall_of(down, own, jnp.where(row < LOW + high, up, blank))
+                at = i * size_x + inner
                 for half in range(2):
                     moved = turned(talls[half], LOW, 1)
-                    start = turned(sides[step_x, 0][half], -2 * index, 1)
-                    end = turned(sides[step_x, 1][half], LOW - 4 * index, 1)
+                    start = turned(sides[step_x, 0][half], LOW - low * (at + 1), 1)
+                    end = turned(sides[step_x, 1][half], LOW - slot * at, 1)
+                    if low < LOW:
+                        start = jnp.where(lane >= LOW - low, start, blank)
                     left = jnp.where(lane < LOW, start, moved)
-                    right = jnp.where(lane < LOW, moved, jnp.where(lane < LOW + HIGH, end, first))
+                    right = jnp.where(lane < LOW, moved, jnp.where(lane < LOW + high, end, blank))
                     if half:
-                        left = jnp.where(row < LOW + HIGH, left, first)
-                        right = jnp.where(row < LOW + HIGH, right, first)
-                    if c == 3:
+                        left = jnp.where(row < LOW + high, left, blank)
+                        right = jnp.where(row < LOW + high, right, blank)
+                    if kind:
                         left, right = lax.rsqrt(left), lax.rsqrt(right)
                     rows = pl.ds(half * size_y, size_y)
-                    fields[c, plane, rows, pl.ds(0, size_z)] = left
-                    fields[c, plane, rows, pl.ds(size_z, size_z)] = right
+                    fields[c, x + LOW, rows, pl.ds(0, size_z)] = left
+                    fields[c, x + LOW, rows, pl.ds(size_z, size_z)] = right
 
     def tables(step_x, step_y, step_z):
         number = slots.index((step_x, step_y, step_z))
@@ -447,9 +460,11 @@
         px = sum_x[2:] + sum_x[:-2] + slope[2:] - slope[:-2]
         slope_x = mx[2:] - mx[:-2]
         sum_y = (2.0 * my + add(my, 2))[1:-1] + my[2:] + my[:-2]
-        py = add(sum_y, 1) + sub(slope_x + slope_z[1:-1], 1)
+        tilt = slope_x + slope_z[1:-1]
+        py = turned(sum_y + tilt, -1, 1) + turned(sum_y - tilt, 1, 1)
         sum_z = (2.0 * mz + add(mz, 1))[1:-1] + mz[2:] + mz[:-2]
-        pz = add(sum_z, 2) + sub(slope_x + slope_y[1:-1], 2)
+        tilt = slope_x + slope_y[1:-1]
+        pz = turned(sum_z + tilt, -1, 2) + turned(sum_z - tilt, 1, 2)
         half = scale[1:-1] * 0.5
         return jnp.stack(
             [half * (m[1:-1] + p * (1.0 / 12.0)) for m, p in ((mx, px), (my, py), (mz, pz))]
@@ -478,8 +493,7 @@
         )
 
     loads[0].wait()
-    loads[1].wait()
-    pack()
+    pack(0)
     loads[2].wait()
     loads[3].wait()
     each = cap // 128
@@ -489,19 +503,20 @@
             for part in range(each):
                 a, b = divmod(at * each + part, 4)
                 nbuf[0, a, pl.ds(b, 1), :] = values[:, part * 128 : part * 128 + 128]
+    loads[1].wait()
+    pack(1)
     for load in loads[4:]:
         load.wait()
     pl.semaphore_wait(barrier, len(peers))
-    go(flows)
-    go(edges)
+    go(halos(0))
     send_round(0)
-    go(scalars)
+    go(halos(1))
     target, stiffness = target_ref[...], stiffness_ref[...]
     live = (lax.broadcasted_iota(jnp.int32, (1, cap), 1) < count_ref[0]).astype(jnp.float32)
     build_main(0, 0)
     edge[...] = jnp.zeros_like(edge)
     wait_halos(0)
-    widen((0, 1, 2), 0.0)
+    widen(0)
     base = live * (target - interpolate(fields[pl.ds(0, 3), pl.ds(1, own_planes)]))
     put(1, base)
     send_round(1)
@@ -513,7 +528,7 @@
         build_side(step_x, step_y, 0)
         build_side(step_x, step_y, 1)
     wait_halos(1)
-    widen((3,), 1.0)
+    widen(1)
     first = apply(1, base)
     send_sum("near", partial_sums(base, first))
     put(2, first)
@@ -559,6 +574,11 @@
     lanes = 2 * size_z
     number, flat = 27, 9
     turns = ITERS + 1
+    halo_shapes = []
+    for parts, low, high, slot in KINDS:
+        more = -(-high * slot // size_y)
+        halo_shapes += [(len(parts), low), (len(parts), slot), (), (), (len(parts), low + high)]
+        halo_shapes += [(len(parts), low + 2), (len(parts), slot + 1 + more), (2, flat)]
     near, far = mesh_counts[1] * mesh_counts[2], mesh_counts[0]
     return pl.pallas_call(
         functools.partial(kernel, mesh_counts, sizes),
@@ -573,14 +593,7 @@
             pltpu.VMEM((1, cap), jnp.float32),
             pltpu.SMEM((1,), jnp.int32),
             pltpu.VMEM((4, WIDE, TALL, lanes), jnp.float32),
-            pltpu.VMEM((4, LOW + HIGH, size_y, size_z), jnp.float32),
-            pltpu.VMEM((4, 2, size_y, size_z), jnp.float32),
-            pltpu.VMEM((4, 4, size_y, size_z), jnp.float32),
-            pltpu.VMEM((4, 4, size_y, size_z), jnp.float32),
-            pltpu.VMEM((4, 7, size_y, size_z), jnp.float32),
-            pltpu.VMEM((size_y, size_z), jnp.float32),
-            pltpu.VMEM((size_y, size_z), jnp.float32),
-            pltpu.VMEM((2, flat, size_y, size_z), jnp.float32),
+            *[pltpu.VMEM(shape + (size_y, size_z), jnp.float32) for shape in halo_shapes],
             pltpu.VMEM((number, 3 * (cap // 256), 4, 128), jnp.float32),
             pltpu.VMEM((ITERS, number, 3, cap // 128, 128), jnp.float32),
             pltpu.VMEM((1, near, 1, 128), jnp.float32),
@@ -598,8 +611,8 @@
             pltpu.SemaphoreType.DMA((turns,)),
             pltpu.SemaphoreType.DMA((4,)),
             pltpu.SemaphoreType.DMA((4,)),
-            pltpu.SemaphoreType.DMA((7,)),
-            pltpu.SemaphoreType.DMA((7,)),
+            pltpu.SemaphoreType.DMA((8,)),
+            pltpu.SemaphoreType.DMA((8,)),
         ],
         compiler_params=pltpu.CompilerParams(
             collective_id=0, has_side_effects=True, vmem_limit_bytes=60 * 1024 * 1024

time: 52 us -> 50.7 us (0.975)
  Pallas kernels: 49.9 us -> 48.6 us
    pallas_call x1, Pallas kernels: 49.9 us -> 48.6 us  [body(): pl.pallas_call(functools.partial(kernel, mesh_counts, sizes), out_shape=j...]
where the time goes in v5:
time: 50.7 us; the launch traced here: 50.6 us
  Pallas kernels  48.6 us (96%)
  local copies, waits for them, and re-layouts  1.28 us (3%)
  between operations  0.66 us (1%)
    pallas_call x1, Pallas kernels, body(): pl.pallas_call(functools.partial(kernel, mesh_counts, sizes), out_shape=j...  48.6 us
    unnamed x1, local copies, waits for them, and re-layouts  1.28 us

profile of v5, /device:TPU:1, one launch (start us, length us, event | category | flops | bytes accessed | tf_op | source)
XLA Modules:
  0.0 50.6 jit_solution(12360844851000581824)
XLA Ops:
  0.7 48.6 %shard_map.73 = f32[3,256]{1,0:T(4,128)} custom-call(f32[8,8,128]{2,1,0:T(8,128)} %density.1, f32[3,8,8,128]{3,2,1,0:T(8,128)} %velocity.1, s32[3,256]{1,0:T(4,128)} %cells_in.1, f32[3,256]{1,0:T(4,128)} %offsets_in.1, f32[3,256]{1,0:T(4,128)} %target_in.1, f32[1,256]{1,0:T(1,128)} %bitcast.1, s32[1]{0:T(128)S(6)} %copy.9.count_in), custom_call_target="tpu_custom_call" | custom-call | tf_op jit(solution)/shard_map/pallas_call | solution.py:583
  49.3 1.3 %copy.10 = f32[3,256]{1,0:T(4,128)} copy(f32[3,256]{1,0:T(4,128)} %shard_map.73) | data formatting | bytes 6144

commit v6 on v5

--- a/solution.py
+++ b/solution.py
@@ -356,7 +356,6 @@
         for plane, product in enumerate(products):
             txy[pl.ds(base + plane * rows, rows), :] = product
         k = FLAT.index((step_x, step_y))
-        used = round_up(size_z + 5, 16)
         high, low = split(table(cell, four, 0, size_z, 0.0, used))
         for ref, part in ((thi, high), (tlo, low)):
             ref[k, pl.ds(0, used), :] = part
@@ -372,8 +371,9 @@
         k = FLAT.index((step_x, step_y))
         tzz[side, k] = table(cell, four, (-1, 1)[side], size_z, float(side * size_z), 8)
 
-    _, own_planes, _, _, _ = PATCHES[0, 0]
+    own_planes = PATCHES[0, 0][1]
     own_rows = own_planes * TALL
+    used = round_up(size_z + 5, 16)
 
     def interpolate(field):
         high, low = split(field.reshape(3 * own_rows, lanes))
@@ -396,14 +396,15 @@
         high, low = split(
             jnp.concatenate([plane * joined(fbuf, turn - 1, number, c) for c in range(3)], axis=0)
         )
-        part = dot_nt(high, thi[k]) + dot_nt(low, thi[k]) + dot_nt(high, tlo[k])
-        part = part.reshape(3, planes, rows, lanes)
+        z_high, z_low = thi[k, pl.ds(0, used), :], tlo[k, pl.ds(0, used), :]
+        part = dot_nt(high, z_high) + dot_nt(low, z_high) + dot_nt(high, z_low)
+        part = part.reshape(3, planes, rows, used)
         if number == 0:
             for edge_plane in (0, WIDE - 1):
                 grid[:, edge_plane] = jnp.zeros((3, TALL, lanes), jnp.float32)
-            grid[:, pl.ds(start, planes)] = part
+            grid[:, pl.ds(start, planes), :, pl.ds(0, used)] = part
         else:
-            grid[:, pl.ds(start, planes), pl.ds(first_row, rows)] += part
+            grid[:, pl.ds(start, planes), pl.ds(first_row, rows), pl.ds(0, used)] += part
 
     def spread_side(turn, step_x, step_y, side):
         start, planes, first_row, rows, base = PATCHES[step_x, step_y]
@@ -438,11 +439,11 @@
             for edge_plane in (0, WIDE - 1):
                 edge[side, edge_plane] = jnp.zeros((TALL, size_z), jnp.float32)
         for step_x, step_y in FLAT:
+            for side in range(2):
+                spread_side(turn, step_x, step_y, side)
+        for step_x, step_y in FLAT:
             if step_x or step_y:
                 spread_main(turn, step_x, step_y)
-        for side in range(2):
-            for step_x, step_y in FLAT:
-                spread_side(turn, step_x, step_y, side)
         finish_sides()
 
     def add(value, axis):
@@ -494,6 +495,8 @@
 
     loads[0].wait()
     pack(0)
+    pl.semaphore_wait(barrier, len(peers))
+    go(halos(0))
     loads[2].wait()
     loads[3].wait()
     each = cap // 128
@@ -503,18 +506,17 @@
             for part in range(each):
                 a, b = divmod(at * each + part, 4)
                 nbuf[0, a, pl.ds(b, 1), :] = values[:, part * 128 : part * 128 + 128]
+    send_round(0)
     loads[1].wait()
     pack(1)
+    go(halos(1))
     for load in loads[4:]:
         load.wait()
-    pl.semaphore_wait(barrier, len(peers))
-    go(halos(0))
-    send_round(0)
-    go(halos(1))
     target, stiffness = target_ref[...], stiffness_ref[...]
     live = (lax.broadcasted_iota(jnp.int32, (1, cap), 1) < count_ref[0]).astype(jnp.float32)
     build_main(0, 0)
     edge[...] = jnp.zeros_like(edge)
+    grid[...] = jnp.zeros_like(grid)
     wait_halos(0)
     widen(0)
     base = live * (target - interpolate(fields[pl.ds(0, 3), pl.ds(1, own_planes)]))

time: 50.7 us -> 50.4 us (level)
  no operation moved by 1% of the time
where the time goes in v6:
time: 50.4 us; the launch traced here: 50.3 us
  Pallas kernels  48.3 us (96%)
  local copies, waits for them, and re-layouts  1.28 us (3%)
  between operations  0.66 us (1%)
    pallas_call x1, Pallas kernels, body(): pl.pallas_call(functools.partial(kernel, mesh_counts, sizes), out_shape=j...  48.3 us
    unnamed x1, local copies, waits for them, and re-layouts  1.28 us

profile of v6, /device:TPU:1, one launch (start us, length us, event | category | flops | bytes accessed | tf_op | source)
XLA Modules:
  0.0 50.3 jit_solution(14135734648680962833)
XLA Ops:
  0.7 48.3 %shard_map.73 = f32[3,256]{1,0:T(4,128)} custom-call(f32[8,8,128]{2,1,0:T(8,128)} %density.1, f32[3,8,8,128]{3,2,1,0:T(8,128)} %velocity.1, s32[3,256]{1,0:T(4,128)} %cells_in.1, f32[3,256]{1,0:T(4,128)} %offsets_in.1, f32[3,256]{1,0:T(4,128)} %target_in.1, f32[1,256]{1,0:T(1,128)} %bitcast.1, s32[1]{0:T(128)S(6)} %copy.9.count_in), custom_call_target="tpu_custom_call" | custom-call | tf_op jit(solution)/shard_map/pallas_call | solution.py:585
  49.0 1.3 %copy.10 = f32[3,256]{1,0:T(4,128)} copy(f32[3,256]{1,0:T(4,128)} %shard_map.73) | data formatting | bytes 6144

commit v7 on v6

--- a/solution.py
+++ b/solution.py
@@ -356,6 +356,10 @@
         for plane, product in enumerate(products):
             txy[pl.ds(base + plane * rows, rows), :] = product
         k = FLAT.index((step_x, step_y))
+        if k:
+            high, low = split(table(cell, four, 0, size_z, 0.0, lanes).T)
+            thi[k], tlo[k] = high, low
+            return
         high, low = split(table(cell, four, 0, size_z, 0.0, used))
         for ref, part in ((thi, high), (tlo, low)):
             ref[k, pl.ds(0, used), :] = part
@@ -396,8 +400,12 @@
         high, low = split(
             jnp.concatenate([plane * joined(fbuf, turn - 1, number, c) for c in range(3)], axis=0)
         )
-        z_high, z_low = thi[k, pl.ds(0, used), :], tlo[k, pl.ds(0, used), :]
-        part = dot_nt(high, z_high) + dot_nt(low, z_high) + dot_nt(high, z_low)
+        if k:
+            dot, where = dot_nn, (k, slice(None), pl.ds(0, used))
+        else:
+            dot, where = dot_nt, (k, pl.ds(0, used), slice(None))
+        z_high, z_low = thi[where], tlo[where]
+        part = dot(high, z_high) + dot(low, z_high) + dot(high, z_low)
         part = part.reshape(3, planes, rows, used)
         if number == 0:
             for edge_plane in (0, WIDE - 1):

time: 50.4 us -> 50.2 us (level)
  no operation moved by 1% of the time
where the time goes in v7:
time: 50.2 us; the launch traced here: 50.1 us
  Pallas kernels  48.1 us (96%)
  local copies, waits for them, and re-layouts  1.28 us (3%)
  between operations  0.66 us (1%)
    pallas_call x1, Pallas kernels, body(): pl.pallas_call(functools.partial(kernel, mesh_counts, sizes), out_shape=j...  48.1 us
    unnamed x1, local copies, waits for them, and re-layouts  1.28 us

profile of v7, /device:TPU:1, one launch (start us, length us, event | category | flops | bytes accessed | tf_op | source)
XLA Modules:
  0.0 50.1 jit_solution(8560555424790695287)
XLA Ops:
  0.7 48.1 %shard_map.73 = f32[3,256]{1,0:T(4,128)} custom-call(f32[8,8,128]{2,1,0:T(8,128)} %density.1, f32[3,8,8,128]{3,2,1,0:T(8,128)} %velocity.1, s32[3,256]{1,0:T(4,128)} %cells_in.1, f32[3,256]{1,0:T(4,128)} %offsets_in.1, f32[3,256]{1,0:T(4,128)} %target_in.1, f32[1,256]{1,0:T(1,128)} %bitcast.1, s32[1]{0:T(128)S(6)} %copy.9.count_in), custom_call_target="tpu_custom_call" | custom-call | tf_op jit(solution)/shard_map/pallas_call | solution.py:593
  48.8 1.3 %copy.10 = f32[3,256]{1,0:T(4,128)} copy(f32[3,256]{1,0:T(4,128)} %shard_map.73) | data formatting | bytes 6144
